TPU v7x, 32 devices: a whole 2x2x4 slice. The times are simulated.
32 devices in a mesh: rep: 4 (over x, y), dp: 8 (over z, core).
Axes of the slice: x: 2, y: 2, z: 4, core: 2. Of those that a mesh axis runs over, the one named last changes fastest.
Arguments:
- x: bfloat16 [32, 2048, 640], P(('rep', 'dp')), parts along dimension 0
- dy: bfloat16 [32, 2048, 640], P(('rep', 'dp')), parts along dimension 0
- w_gate: bfloat16 [2, 640, 2560], replicated
- w_up: bfloat16 [2, 640, 2560], replicated
- w_down: bfloat16 [2, 2560, 640], replicated
- m_w_gate: float32 [2, 640, 2560], P(None, 'dp')
- m_w_up: float32 [2, 640, 2560], P(None, 'dp')
- m_w_down: float32 [2, 2560, 640], P(None, 'dp')
- v_w_gate: float32 [2, 640, 2560], P(None, 'dp')
- v_w_up: float32 [2, 640, 2560], P(None, 'dp')
- v_w_down: float32 [2, 2560, 640], P(None, 'dp')
Outputs:
- output 1: bfloat16 [8, 640, 2560], P('rep'), parts along dimension 0
- output 2: bfloat16 [8, 640, 2560], P('rep'), parts along dimension 0
- output 3: bfloat16 [8, 2560, 640], P('rep'), parts along dimension 0
- output 4: float32 [8, 640, 2560], P('rep', 'dp'), parts along dimension 0
- output 5: float32 [8, 640, 2560], P('rep', 'dp'), parts along dimension 0
- output 6: float32 [8, 2560, 640], P('rep', 'dp'), parts along dimension 0
- output 7: float32 [8, 640, 2560], P('rep', 'dp'), parts along dimension 0
- output 8: float32 [8, 640, 2560], P('rep', 'dp'), parts along dimension 0
- output 9: float32 [8, 2560, 640], P('rep', 'dp'), parts along dimension 0
There are 4 independent parts. A program takes and returns all parts, laid end to end along the dimension named above; an argument that names none is the same for every part.
All inputs are finite; a program needn't handle non-finite values.
Results may differ from a plain program's by a relative error of at most 0.022.
Values are sent between devices in bfloat16 or wider.
A program may use at most 2 GiB of HBM per device.

v0:
```python
import jax
import jax.numpy as jnp
from jax import lax

NAMES = ("w_gate", "w_up", "w_down")


def matmul(a, w):
    return jnp.dot(a, w, preferred_element_type=jnp.float32).astype(jnp.bfloat16)


def normed(h):
    wide = h.astype(jnp.float32)
    scale = lax.rsqrt(jnp.mean(wide**2, -1, keepdims=True) + 1e-6)
    return (wide * scale).astype(jnp.bfloat16)


def layer(h, w):
    a = normed(h)
    gate = jnp.dot(a, w["w_gate"], preferred_element_type=jnp.float32)
    up = jnp.dot(a, w["w_up"], preferred_element_type=jnp.float32)
    return h + matmul((jax.nn.silu(gate) * up).astype(jnp.bfloat16), w["w_down"])


def adamw(w, m, v, g):
    m = 0.9 * m + 0.1 * g
    v = 0.95 * v + 0.05 * g * g
    step = m * lax.rsqrt(v + 1e-8) + 0.1 * w
    return (w - 0.02 * step).astype(jnp.bfloat16), m, v


def clipped(gradients, sum_of_squares, count):
    factor = jnp.minimum(1.0, 0.5 * lax.rsqrt(sum_of_squares / count + 1e-30))
    return [g * factor for g in gradients]


def stack(weights, h):
    for number in range(weights["w_gate"].shape[0]):
        h = layer(h, {name: w[number] for name, w in weights.items()})
    return h


def solution(mesh):
    groups = mesh.shape["rep"]

    def step(x, dy, *arrays):
        weights, m, v = (arrays[i : i + 3] for i in (0, 3, 6))
        x, dy = (t.reshape(groups, -1, *t.shape[1:]) for t in (x, dy))

        def of_a_group(x, dy):
            _, back = jax.vjp(lambda w: stack(w, x), dict(zip(NAMES, weights, strict=True)))
            by_weights = back(dy)[0]
            gradients = [by_weights[name].astype(jnp.float32) for name in NAMES]
            gradients = clipped(gradients, sum(jnp.sum(g * g) for g in gradients), sum(g.size for g in gradients))
            new = [adamw(w.astype(jnp.float32), m, v, g) for w, m, v, g in zip(weights, m, v, gradients, strict=True)]
            return tuple(one[which] for which in range(3) for one in new)

        return tuple(t.reshape(-1, *t.shape[2:]) for t in jax.vmap(of_a_group)(x, dy))

    return step
```

profile of v0, /device:TPU:0, one launch (start us, length us, event | category | flops | bytes accessed | tf_op | source)
XLA Modules:
  0.0 813.5 jit_solution(4539326121594878227)
XLA Ops:
  24.5 16.3 %fusion.65 = f32[2048,2560]{1,0:T(8,128)} fusion(bf16[2,640,2560]{2,1,0:T(8,128)(2,1)} %param.3, bf16[1,2048,640]{2,1,0:T(8,128)(2,1)S(1)} %copy-done.1, f32[2048]{0:T(1024)S(1)} %add_rsqrt_fusion), kind=kOutput, calls=%fused_computation.77 | convolution fusion | flops 6714818560 | bytes 26877952 | tf_op jit(solution)/vmap(jvp())/dot_general | solution.py:21
  40.8 15.6 %fusion.26 = bf16[2048,2560]{1,0:T(8,128)(2,1)} fusion(f32[2048,2560]{1,0:T(8,128)} %fusion.65, f32[2048,2560]{1,0:T(8,128)S(1)} %fusion.67), kind=kLoop, calls=%fused_computation.37 | loop fusion | flops 31457280 | bytes 52428800
  56.4 11.2 %fusion.51 = (f32[2048]{0:T(1024)S(1)}, bf16[1,1,2048,640]{2,3,1,0:T(8,128)(2,1)S(1)}) fusion(bf16[2048,2560]{1,0:T(8,128)(2,1)} %fusion.26, bf16[2,2560,640]{2,1,0:T(8,128)(2,1)} %param.4, bf16[1,2048,640]{1,2,0:T(8,128)(2,1)S(1)} %copy-done.9), kind=kOutput, calls=%fused_computation.62 | convolution fusion | flops 6717437952 | bytes 19013632 | tf_op jit(solution)/vmap(jvp())/dot_general | solution.py:9
  68.3 13.6 %fusion.54 = f32[2048,2560]{1,0:T(8,128)} fusion(bf16[2,640,2560]{2,1,0:T(8,128)(2,1)} %param, bf16[1,1,2048,640]{2,3,1,0:T(8,128)(2,1)S(1)} %get-tuple-element.10, f32[2048]{0:T(1024)S(1)} %bitcast.355), kind=kOutput, calls=%fused_computation.66 | convolution fusion | flops 6714818560 | bytes 26877952 | tf_op jit(solution)/vmap(jvp())/dot_general | solution.py:20
  81.9 13.6 %fusion.58 = f32[2048,2560]{1,0:T(8,128)} fusion(bf16[2,640,2560]{2,1,0:T(8,128)(2,1)} %param.3, bf16[1,1,2048,640]{2,3,1,0:T(8,128)(2,1)S(1)} %get-tuple-element.10, f32[2048]{0:T(1024)S(1)} %bitcast.356), kind=kOutput, calls=%fused_computation.70 | convolution fusion | flops 6714818560 | bytes 26877952 | tf_op jit(solution)/vmap(jvp())/dot_general | solution.py:21
  95.5 19.5 %fusion.35 = f32[1,2560,640]{2,1,0:T(8,128)} fusion(f32[2048,2560]{1,0:T(8,128)} %fusion.58, f32[2048,2560]{1,0:T(8,128)} %fusion.54, bf16[1,2048,640]{2,1,0:T(8,128)(2,1)S(1)} %copy-done.8), kind=kOutput, calls=%fused_computation.52 | convolution fusion | flops 6742343680 | bytes 51118080 | tf_op jit(solution)/vmap(transpose(jvp()))/dot_general | solution.py:9
  118.5 10.9 %convolution_convert_fusion.1 = bf16[2048,2560]{1,0:T(8,128)(2,1)S(1)} fusion(bf16[2,2560,640]{2,1,0:T(8,128)(2,1)} %param.4, bf16[1,2048,640]{2,1,0:T(8,128)(2,1)} %param.5), kind=kOutput, calls=%fused_computation.36 | convolution fusion | flops 6716129280 | bytes 16384000 | tf_op jit(solution)/vmap(transpose(jvp()))/dot_general | solution.py:9
  133.3 20.2 %fusion.6 = bf16[2048,2560]{1,0:T(8,128)(2,1)} fusion(f32[2048,2560]{1,0:T(8,128)} %fusion.54, f32[2048,2560]{1,0:T(8,128)} %fusion.58, bf16[2048,2560]{1,0:T(8,128)(2,1)S(1)} %convolution_convert_fusion.1), kind=kLoop, calls=%fused_computation.11 | loop fusion | flops 62914560 | bytes 62914560
  153.5 15.7 %fusion.78 = bf16[2048,640]{0,1:T(8,128)(2,1)} fusion(bf16[2048,2560]{1,0:T(8,128)(2,1)} %copy-done.2, f32[2048,2560]{1,0:T(8,128)} %fusion.54, bf16[2,640,2560]{2,1,0:T(8,128)(2,1)} %param.3), kind=kOutput, calls=%fused_computation.86 | convolution fusion | flops 6743654400 | bytes 37355520 | tf_op jit(solution)/vmap(transpose(jvp()))/dot_general | solution.py:21
  169.2 13.5 %fusion.53 = (f32[2048]{0:T(1024)S(1)}, bf16[2048,640]{0,1:T(8,128)(2,1)S(1)}) fusion(bf16[1,1,2048,640]{2,3,1,0:T(8,128)(2,1)} %copy-done.4, bf16[2048,640]{0,1:T(8,128)(2,1)} %fusion.78, bf16[2048,2560]{1,0:T(8,128)(2,1)} %fusion.6, bf16[2,640,2560]{2,1,0:T(8,128)(2,1)} %param), kind=kOutput, calls=%fused_computation.64 | convolution fusion | flops 6717437952 | bytes 21635072 | tf_op jit(solution)/vmap(transpose(jvp()))/dot_general | solution.py:20
  186.1 12.8 %convolution_bitcast_fusion = f32[1,2560,640]{2,1,0:T(8,128)} fusion(bf16[2048,2560]{1,0:T(8,128)(2,1)} %fusion.26, bf16[2048,640]{0,1:T(8,128)(2,1)S(1)} %fusion.95), kind=kOutput, calls=%fused_computation.56 | convolution fusion | flops 6710886400 | bytes 19660800 | tf_op jit(solution)/vmap(transpose(jvp()))/dot_general | solution.py:9
  200.6 15.7 %fusion.38 = f32[1,640,2560]{2,1,0:T(8,128)} fusion(bf16[2048,2560]{1,0:T(8,128)(2,1)} %copy-done.2, f32[2048,2560]{1,0:T(8,128)} %fusion.54, bf16[1,1,2048,640]{2,3,1,0:T(8,128)(2,1)S(1)} %copy-done.6, f32[2048]{0:T(1024)S(1)} %bitcast.358), kind=kOutput, calls=%fused_computation.53 | convolution fusion | flops 6746275840 | bytes 40640512 | tf_op jit(solution)/vmap(transpose(jvp()))/dot_general | solution.py:21
  216.5 13.7 %convolution_convert_fusion = bf16[2048,2560]{1,0:T(8,128)(2,1)} fusion(bf16[2048,640]{0,1:T(8,128)(2,1)} %copy-done.7, bf16[2,2560,640]{2,1,0:T(8,128)(2,1)} %param.4), kind=kOutput, calls=%fused_computation.35 | convolution fusion | flops 6716129280 | bytes 16384000 | tf_op jit(solution)/vmap(transpose(jvp()))/dot_general | solution.py:9
  230.1 15.8 %fusion.44 = f32[1,640,2560]{2,1,0:T(8,128)} fusion(bf16[2048,2560]{1,0:T(8,128)(2,1)} %convolution_convert_fusion, f32[2048,2560]{1,0:T(8,128)} %copy-done, bf16[1,2048,640]{1,2,0:T(8,128)(2,1)S(1)} %copy-done.10, f32[2048]{0:T(1024)S(1)} %copy-done.15), kind=kOutput, calls=%fused_computation.55 | convolution fusion | flops 6746275840 | bytes 40640512 | tf_op jit(solution)/vmap(transpose(jvp()))/dot_general | solution.py:21
  246.0 11.3 %convolution_bitcast_fusion.1 = f32[1,640,2560]{2,1,0:T(8,128)} fusion(bf16[2048,2560]{1,0:T(8,128)(2,1)} %fusion.6, bf16[1,1,2048,640]{2,3,1,0:T(8,128)(2,1)S(1)} %copy-done.6, f32[2048]{0:T(1024)S(1)} %bitcast.359), kind=kOutput, calls=%fused_computation.57 | convolution fusion | flops 6714818560 | bytes 19668992 | tf_op jit(solution)/vmap(transpose(jvp()))/dot_general | solution.py:20
  259.0 22.6 %fusion.41 = f32[1,640,2560]{2,1,0:T(8,128)} fusion(f32[2048,2560]{1,0:T(8,128)} %copy-done, f32[2048,2560]{1,0:T(8,128)} %fusion.65, bf16[2048,2560]{1,0:T(8,128)(2,1)} %convolution_convert_fusion, bf16[1,2048,640]{1,2,0:T(8,128)(2,1)S(1)} %copy-done.11, f32[2048]{0:T(1024)S(1)} %copy-done.15), kind=kOutput, calls=%fused_computation.54 | convolution fusion | flops 6772490240 | bytes 61612032 | tf_op jit(solution)/vmap(transpose(jvp()))/dot_general | solution.py:20
  287.0 60.0 %reduce-scatter.23.cloned.1.call-done = f32[1,80,2560]{2,1,0:T(8,128)} async-done(((f32[1,640,2560]{2,1,0:T(8,128)}), f32[1,80,2560]{2,1,0:T(8,128)}) %reduce-scatter.23.cloned.1.call-update) | async-done | bytes 819216
  348.2 72.4 %reduce-scatter.25.cloned.1.call-done = f32[1,80,2560]{2,1,0:T(8,128)} async-done(((f32[1,640,2560]{2,1,0:T(8,128)}), f32[1,80,2560]{2,1,0:T(8,128)}) %reduce-scatter.25.cloned.1.call-update) | async-done | bytes 819216
  422.9 71.4 %reduce-scatter.19.cloned.1.call-done = f32[1,80,2560]{2,1,0:T(8,128)} async-done(((f32[1,640,2560]{2,1,0:T(8,128)}), f32[1,80,2560]{2,1,0:T(8,128)}) %reduce-scatter.19.cloned.1.call-update) | async-done | bytes 819216
  495.4 72.4 %reduce-scatter.21.cloned.1.call-done = f32[1,80,2560]{2,1,0:T(8,128)} async-done(((f32[1,640,2560]{2,1,0:T(8,128)}), f32[1,80,2560]{2,1,0:T(8,128)}) %reduce-scatter.21.cloned.1.call-update) | async-done | bytes 819216
  572.0 14.9 %all-reduce.16 = f32[1]{0:T(128)} all-reduce(f32[1]{0:T(128)} %bitcast.50), channel_id=5, replica_groups=mesh['rep'=4,'dp'=8] {'dp'}, use_global_device_ids=true, to_apply=%region_3.4.clone | all-reduce | flops 1 | bytes 8 | tf_op jit(solution)/vmap()/reduce_sum | solution.py:54
  603.0 54.5 %all-gather.14.cloned.1.call-done = bf16[1,2,2560,640]{3,2,1,0:T(8,128)(2,1)} async-done(((bf16[1,2,320,640]{3,2,1,0:T(8,128)(2,1)}), bf16[1,2,2560,640]{3,2,1,0:T(8,128)(2,1)}) %all-gather.14.cloned.1.call-update) | async-done | bytes 6553616 | tf_op jit(solution)/reshape | solution.py:58
  657.5 67.4 %all-gather.10.cloned.1.call-done = bf16[1,2,640,2560]{3,2,1,0:T(8,128)(2,1)} async-done(((bf16[1,2,80,2560]{3,2,1,0:T(8,128)(2,1)}), bf16[1,2,640,2560]{3,2,1,0:T(8,128)(2,1)}) %all-gather.10.cloned.1.call-update) | async-done | bytes 6553616 | tf_op jit(solution)/reshape | solution.py:58
  724.8 67.4 %all-gather.12.cloned.1.call-done = bf16[1,2,640,2560]{3,2,1,0:T(8,128)(2,1)} async-done(((bf16[1,2,80,2560]{3,2,1,0:T(8,128)(2,1)}), bf16[1,2,640,2560]{3,2,1,0:T(8,128)(2,1)}) %all-gather.12.cloned.1.call-update) | async-done | bytes 6553616 | tf_op jit(solution)/reshape | solution.py:58
  (84 shorter events, 73.3 us)
Async XLA Ops:
  7.2 6.9 copy-start.1
  7.2 276.4 %reduce-scatter.27.cloned.1.call-start = ((), (), s32[]{:S(2)}) async-start(), calls=%async_computation.13 | async-start | bytes 7372800
  14.1 10.4 %copy-start.14 = (f32[2048]{0:T(1024)}, f32[2048]{0:T(1024)S(1)}, u32[]{:S(2)}) copy-start(f32[2048]{0:T(1024)S(1)} %add_rsqrt_fusion) | copy-start | bytes 24580
  24.5 16.3 %copy-start = (f32[2048,2560]{1,0:T(8,128)}, f32[2048,2560]{1,0:T(8,128)S(1)}, u32[]{:S(2)}) copy-start(f32[2048,2560]{1,0:T(8,128)S(1)} %fusion.67) | copy-start | bytes 62914564
  40.8 15.6 %copy-start.9 = (bf16[1,2048,640]{1,2,0:T(8,128)(2,1)S(1)}, bf16[1,2048,640]{1,2,0:T(8,128)(2,1)}, u32[]{:S(2)}) copy-start(bf16[1,2048,640]{1,2,0:T(8,128)(2,1)} %copy) | copy-start | bytes 7864324
  67.6 14.3 %copy-start.4 = (bf16[1,1,2048,640]{2,3,1,0:T(8,128)(2,1)}, bf16[1,1,2048,640]{2,3,1,0:T(8,128)(2,1)S(1)}, u32[]{:S(2)}) copy-start(bf16[1,1,2048,640]{2,3,1,0:T(8,128)(2,1)S(1)} %get-tuple-element.10) | copy-start | bytes 7864324
  81.9 13.6 %copy-start.8 = (bf16[1,2048,640]{2,1,0:T(8,128)(2,1)S(1)}, bf16[1,2048,640]{2,1,0:T(8,128)(2,1)}, u32[]{:S(2)}) copy-start(bf16[1,2048,640]{2,1,0:T(8,128)(2,1)} %param.5) | copy-start | bytes 7864324
  115.1 169.8 %reduce-scatter.29.cloned.1.call-start = ((), (), s32[]{:S(2)}) async-start(), calls=%async_computation.14 | async-start | bytes 7372800
  129.4 4.0 copy-start.2
  169.2 13.5 %copy-start.13 = (f32[2048]{0:T(1024)S(1)}, f32[2048]{0:T(1024)}, u32[]{:S(2)}) copy-start(f32[2048]{0:T(1024)} %copy-done.12) | copy-start | bytes 24580
  169.2 13.5 %copy-start.5 = (bf16[1,1,2048,640]{2,3,1,0:T(8,128)(2,1)S(1)}, bf16[1,1,2048,640]{2,3,1,0:T(8,128)(2,1)}, u32[]{:S(2)}) copy-start(bf16[1,1,2048,640]{2,3,1,0:T(8,128)(2,1)} %copy-done.4) | copy-start | bytes 7864324
  198.9 1.7 copy-start.6
  198.9 148.1 %reduce-scatter.23.cloned.1.call-start = ((), (), s32[]{:S(2)}) async-start(), calls=%async_computation.11 | async-start | bytes 7372800
  216.4 13.7 %copy-start.15 = (f32[2048]{0:T(1024)S(1)}, f32[2048]{0:T(1024)}, u32[]{:S(2)}) copy-start(f32[2048]{0:T(1024)} %copy-done.14) | copy-start | bytes 24580
  216.4 204.2 %reduce-scatter.25.cloned.1.call-start = ((), (), s32[]{:S(2)}) async-start(), calls=%async_computation.12 | async-start | bytes 7372800
  216.5 13.7 %copy-start.10 = (bf16[1,2048,640]{1,2,0:T(8,128)(2,1)S(1)}, bf16[1,2048,640]{1,2,0:T(8,128)(2,1)}, u32[]{:S(2)}) copy-start(bf16[1,2048,640]{1,2,0:T(8,128)(2,1)} %copy) | copy-start | bytes 7864324
  245.9 248.3 %reduce-scatter.19.cloned.1.call-start = ((), (), s32[]{:S(2)}) async-start(), calls=%async_computation.9 | async-start | bytes 7372800
  257.3 310.5 %reduce-scatter.21.cloned.1.call-start = ((), (), s32[]{:S(2)}) async-start(), calls=%async_computation.10 | async-start | bytes 7372800
  281.7 375.8 %all-gather.14.cloned.1.call-start = ((), (), s32[]{:S(2)}) async-start(), calls=%async_computation.8 | async-start | bytes 7372800 | tf_op jit(solution)/reshape | solution.py:58
  592.7 132.1 %all-gather.10.cloned.1.call-start = ((), (), s32[]{:S(2)}) async-start(), calls=%async_computation.6 | async-start | bytes 7372800 | tf_op jit(solution)/reshape | solution.py:58
  597.9 194.4 %all-gather.12.cloned.1.call-start = ((), (), s32[]{:S(2)}) async-start(), calls=%async_computation.7 | async-start | bytes 7372800 | tf_op jit(solution)/reshape | solution.py:58
  792.2 6.8 copy-start.3
  792.2 10.1 %slice-start = ((s8[6553600]{0:T(1024)(128)(4,1)}), s8[4194304]{0:T(1024)(128)(4,1)S(1)}, s32[]{:S(2)}) async-start(s8[6553600]{0:T(1024)(128)(4,1)} %bitcast.347), calls=%async_computation.15 | async-start | bytes 8388608
  799.0 4.7 slice-start.1
  (4 other events, 4.5 us)
Sparse Core Ops, SparseCore 0:
  115.2 74.7 reduce-scatter.26
  199.0 74.7 reduce-scatter.28
  276.2 70.8 reduce-scatter.22
  349.8 70.8 reduce-scatter.24
  423.4 70.8 reduce-scatter.18
  497.0 70.8 reduce-scatter.20
  592.9 64.5 all-gather.13
  659.7 65.1 all-gather.9
  727.0 65.1 all-gather.11
where the time goes:
time: 822 us; the launch traced here: 813 us
  waiting for transfers between devices  466 us (57%)
  matrix products  217 us (26%)
  other arithmetic  65.4 us (8%)
  local copies, waits for them, and re-layouts  32.7 us (4%)
  between operations  17.8 us (2%)
  blocking collectives  14.9 us (2%)
    unnamed x15, waiting for transfers between devices  276 us
    reshape x3, waiting for transfers between devices, step(): t.reshape(-1, *t.shape[2:])  189 us
    dot_general x5, matrix products, layer(): up = jnp.dot(a, w['w_up'], preferred_element_type=jnp.float32)  77.1 us
    dot_general x5, matrix products, layer(): gate = jnp.dot(a, w['w_gate'], preferred_element_type=jnp.float32)  71.4 us
    dot_general x5, matrix products, matmul(): jnp.dot(a, w, preferred_element_type=jnp.float32).astype(jnp.bfloat16)  68.1 us
    unnamed x4, other arithmetic  37.5 us
    unnamed x43, local copies, waits for them, and re-layouts  32.1 us
  transfers between devices with their start and end apart: 9, of which 7 were waited for; matrix products, arithmetic and copies ran while one was open for 22% of the time, Pallas kernels for 0%

commit v1 on v0

v1 whole, which is shorter than its diff:
```python
import functools

import jax
import jax.numpy as jnp
from jax import lax
from jax.experimental import pallas as pl
from jax.experimental.pallas import tpu as pltpu
from jax.sharding import PartitionSpec as P

f32, bf16 = jnp.float32, jnp.bfloat16
D, F, Q = 640, 2560, 640
LAYERS = 2
ITEMS = 8
SLOTS = 5
TM = 512
COLS = ((0, 256), (256, 256), (512, 128))


def dot(a, b):
    return jnp.dot(a, b, preferred_element_type=f32)


def dot_bt(a, b):
    return lax.dot_general(a, b, (((1,), (1,)), ((), ())), preferred_element_type=f32)


def dot_at(a, b):
    return lax.dot_general(a, b, (((0,), (0,)), ((), ())), preferred_element_type=f32)


def rows(t, n):
    return pl.ds(pl.multiple_of(t * n, n), n)


def loop(n, body):
    lax.fori_loop(0, n, lambda i, _: (body(i), 0)[1], 0)


def place():
    me = lax.axis_index("dp")
    return me, lax.div(me, 2), lax.rem(me, 2)


def quarter(i):
    r = lax.rem(i, 4)
    odd, half = lax.rem(r, 2), lax.div(r, 2)
    return (1 - odd) * (2 + half) + odd * (1 - half)


def step_kernel(
    x, dy, wg, wu, wd, og, ou, od, oss,
    h_v, a_v, dy_v, big, da_v, wgu_v, wdb_v, wda_v, own, ownd, pair, paird, got, gotd, ss_v,
    in_sem, w_sem, psend, precv, ssend, srecv, fsem, credit, pcredit,
):
    tokens = x.shape[0]
    me, z, c = place()
    partner = {"dp": me + 1 - 2 * c}

    def weights(l, q, slot, down=True):
        cols = rows(q, Q)
        two = (
            pltpu.make_async_copy(wg.at[l, :, cols], wgu_v.at[slot, :, 0:Q], w_sem.at[slot, 0]),
            pltpu.make_async_copy(wu.at[l, :, cols], wgu_v.at[slot, :, Q : 2 * Q], w_sem.at[slot, 1]),
        )
        return two + (pltpu.make_async_copy(wd.at[l, cols], wdb_v.at[slot], w_sem.at[slot, 2]),) if down else two

    load_x = pltpu.make_async_copy(x, h_v, in_sem.at[0])
    load_dy = pltpu.make_async_copy(dy, dy_v, in_sem.at[1])
    load_wd = pltpu.make_async_copy(wd.at[0], wda_v, in_sem.at[2])
    load_x.start()
    for copy in weights(0, 0, 0, False):
        copy.start()
    load_wd.start()
    load_dy.start()

    ss_v[...] = jnp.zeros_like(ss_v)
    got[...] = jnp.zeros_like(got)
    gotd[...] = jnp.zeros_like(gotd)
    barrier = pltpu.get_barrier_semaphore()
    pl.semaphore_signal(barrier, inc=1, device_id=partner)

    @pl.when(z > 0)
    def _():
        pl.semaphore_signal(barrier, inc=1, device_id={"dp": me - 2})

    @pl.when(z < 3)
    def _():
        pl.semaphore_signal(barrier, inc=1, device_id={"dp": me + 2})

    def zero(t):
        da_v[rows(t, 128)] = jnp.zeros((128, D), f32)

    loop(tokens // 128, zero)
    load_x.wait()

    def norm(l):
        def tile(t):
            r = rows(t, 256)
            wide = h_v[r].astype(f32)
            a_v[l, r] = (wide * lax.rsqrt(jnp.mean(wide * wide, -1, keepdims=True) + 1e-6)).astype(bf16)

        loop(tokens // 256, tile)

    norm(0)

    def forward(n):
        slot = lax.rem(n, 2)
        for copy in weights(0, n, slot, False):
            copy.wait()

        @pl.when(n < 3)
        def _():
            for copy in weights(0, n + 1, 1 - slot, False):
                copy.start()

        def tile(t):
            r = rows(t, TM)
            a = a_v[0, r]
            for c0, cn in COLS:
                g = dot(a, wgu_v[slot, :, c0 : c0 + cn])
                u = dot(a, wgu_v[slot, :, Q + c0 : Q + c0 + cn])
                big[r, pl.ds(pl.multiple_of(n * Q + c0, 128), cn)] = (g / (1 + jnp.exp(-g)) * u).astype(bf16)

        loop(tokens // TM, tile)

    loop(4, forward)
    for copy in weights(1, quarter(0), 0):
        copy.start()
    load_wd.wait()

    def down(t):
        r = rows(t, TM)
        h_v[r] = h_v[r] + dot(big[r], wda_v[...]).astype(bf16)

    loop(tokens // TM, down)
    norm(1)
    load_dy.wait()
    near = 2 + lax.convert_element_type((z > 0) & (z < 3), jnp.int32)
    pl.semaphore_wait(barrier, near)

    def item_of(s, way):
        return (1 - way) * (s - 1 - z) + way * (s - 4 + z)

    def is_last(way):
        return z == 3 * (1 - way)

    def is_first(way):
        return z == 3 * way

    def has_d(i, way):
        return lax.rem(i, 2) == way

    def send_gu(way, i, b):
        slot, r = lax.rem(i, SLOTS), lax.rem(i, 2)
        return pltpu.make_async_remote_copy(
            own.at[slot, 2 * (1 - way) + b, c], got.at[way, r, b], ssend.at[way, slot, b], srecv.at[way, r, b],
            device_id={"dp": me + 2 - 4 * way},
        )

    def send_d(way, i):
        slot, r = lax.rem(i, SLOTS), lax.rem(i, 2)
        return pltpu.make_async_remote_copy(
            ownd.at[slot, c], gotd.at[r], ssend.at[way, slot, 2], srecv.at[way, r, 2],
            device_id={"dp": me + 2 - 4 * way},
        )

    def keep_gu(way, i, b):
        slot, q = lax.rem(i, SLOTS), quarter(i)
        j, l = way * b + (1 - way) * (1 - b), 1 - lax.div(i, 4)
        src = own.at[slot, 2 * (1 - way) + b, c]
        return (
            pltpu.make_async_copy(src.at[:, 0:Q], og.at[j, l, :, rows(q, Q)], fsem.at[slot, 2 * b]),
            pltpu.make_async_copy(src.at[:, Q : 2 * Q], ou.at[j, l, :, rows(q, Q)], fsem.at[slot, 2 * b + 1]),
        )

    def keep_d(way, i):
        slot, q = lax.rem(i, SLOTS), quarter(i)
        j, l = way * q + (1 - way) * (3 - q), 1 - lax.div(i, 4)
        return pltpu.make_async_copy(ownd.at[slot, c], od.at[j, l], fsem.at[slot, 4])

    def swap(i):
        slot = lax.rem(i, SLOTS)
        return (
            pltpu.make_async_remote_copy(own.at[slot, :, 1 - c], pair.at[slot], psend.at[slot, 0], precv.at[slot, 0], device_id=partner),
            pltpu.make_async_remote_copy(ownd.at[slot, 1 - c], paird.at[slot], psend.at[slot, 1], precv.at[slot, 1], device_id=partner),
        )

    def settle(i):
        for copy in swap(i):
            copy.wait_send()

        def one(way):
            @pl.when(is_last(way))
            def _():
                for b in range(2):
                    for copy in keep_gu(way, i, b):
                        copy.wait()

                @pl.when(has_d(i, way))
                def _():
                    keep_d(way, i).wait()

            @pl.when(jnp.logical_not(is_last(way)))
            def _():
                for b in range(2):
                    send_gu(way, i, b).wait_send()

                @pl.when(has_d(i, way))
                def _():
                    send_d(way, i).wait_send()

        loop(2, one)

    def stage(way, i):
        slot, r = lax.rem(i, SLOTS), lax.rem(i, 2)

        @pl.when(jnp.logical_not(is_last(way)) & (i >= 2))
        def _():
            pl.semaphore_wait(credit.at[way], 1)

        def gu(b):
            @pl.when(jnp.logical_not(is_first(way)))
            def _():
                send_gu(way, i, b).wait_recv()

            zb = 2 * (1 - way) + b

            def part(k):
                at = rows(k, 16)
                total = own[slot, zb, c, at].astype(f32) + pair[slot, zb, at].astype(f32) + got[way, r, b, at].astype(f32)
                total = total.astype(bf16)
                own[slot, zb, c, at] = total

                @pl.when(is_last(way))
                def _():
                    g = total.astype(f32)
                    ss_v[...] += jnp.sum((g * g).reshape(2, 8, 2 * Q), 0)

            loop(5, part)

            @pl.when(is_last(way))
            def _():
                for copy in keep_gu(way, i, b):
                    copy.start()

            @pl.when(jnp.logical_not(is_last(way)))
            def _():
                send_gu(way, i, b).start()

        loop(2, gu)

        @pl.when(has_d(i, way))
        def _():
            @pl.when(jnp.logical_not(is_first(way)))
            def _():
                send_d(way, i).wait_recv()

            def part(k):
                at = rows(k, 32)
                other = jnp.where(is_first(way), 0.0, gotd[r, at].astype(f32))
                total = (ownd[slot, c, at].astype(f32) + paird[slot, at].astype(f32) + other).astype(bf16)
                ownd[slot, c, at] = total

                @pl.when(is_last(way))
                def _():
                    g = total.astype(f32)
                    ss_v[:, 0:D] += jnp.sum((g * g).reshape(4, 8, D), 0)

            loop(10, part)

            @pl.when(is_last(way))
            def _():
                keep_d(way, i).start()

            @pl.when(jnp.logical_not(is_last(way)))
            def _():
                send_d(way, i).start()

        @pl.when(jnp.logical_not(is_first(way)) & (i < ITEMS - 2))
        def _():
            pl.semaphore_signal(credit.at[way], inc=1, device_id={"dp": me - 2 + 4 * way})

    def engine(s):
        @pl.when((s >= 1) & (s <= ITEMS))
        def _():
            for copy in swap(s - 1):
                copy.wait_recv()

        def one(way):
            i = item_of(s, way)

            @pl.when((i >= 0) & (i < ITEMS))
            def _():
                stage(way, i)

        loop(2, one)

        @pl.when((s >= SLOTS - 1) & (s < ITEMS - 1))
        def _():
            pl.semaphore_signal(pcredit, inc=1, device_id=partner)

    def backward_norm():
        def tile(t):
            r = rows(t, 256)
            wide, da = h_v[r].astype(f32), da_v[r].astype(bf16).astype(f32)
            scale = lax.rsqrt(jnp.mean(wide * wide, -1, keepdims=True) + 1e-6)
            dot_mean = jnp.mean(da * wide, -1, keepdims=True)
            dwide = scale * da - wide * (scale * scale * scale * dot_mean)
            dy_v[r] = (dy_v[r].astype(f32) + dwide.astype(bf16).astype(f32)).astype(bf16)

        loop(tokens // 256, tile)

    def step(s):
        l, slot, at = 1 - lax.div(s, 4), lax.rem(s, SLOTS), lax.rem(s, 2)

        @pl.when(s < ITEMS)
        def _():
            for copy in weights(l, quarter(s), at):
                copy.wait()

            @pl.when(s < ITEMS - 1)
            def _():
                for copy in weights(1 - lax.div(s + 1, 4), quarter(s + 1), 1 - at):
                    copy.start()

            @pl.when(s == 4)
            def _():
                backward_norm()

            def tile(t):
                r = rows(t, TM)
                a, dh = a_v[l, r], dy_v[r]
                for c0, cn in COLS:
                    g = dot(a, wgu_v[at, :, c0 : c0 + cn])
                    u = dot(a, wgu_v[at, :, Q + c0 : Q + c0 + cn])
                    d = dot_bt(dh, wdb_v[at, c0 : c0 + cn]).astype(bf16).astype(f32)
                    sig = 1 / (1 + jnp.exp(-g))
                    silu = g * sig
                    big[r, 2 * Q + c0 : 2 * Q + c0 + cn] = (silu * u).astype(bf16)
                    big[r, Q + c0 : Q + c0 + cn] = (d * silu).astype(bf16)
                    big[r, c0 : c0 + cn] = (d * u * (sig + silu * (1 - sig))).astype(bf16)

            loop(tokens // TM, tile)

        engine(s)

        @pl.when(s < ITEMS)
        def _():
            @pl.when(s >= SLOTS)
            def _():
                settle(s - SLOTS)
                pl.semaphore_wait(pcredit, 1)

            for n in range(5):
                k = 128 * n
                value = dot_at(big[:, 2 * Q + k : 2 * Q + k + 128], dy_v[...]).astype(bf16)
                for half in range(2):
                    lo, hi = max(k, 320 * half), min(k + 128, 320 * half + 320)
                    if lo < hi:
                        ownd[slot, half, lo - 320 * half : hi - 320 * half] = value[lo - k : hi - k]

            def cols(n):
                k = pl.ds(pl.multiple_of(n * 256, 256), 256)
                own[slot, :, :, :, k] = dot_at(a_v[l], big[:, k]).astype(bf16).reshape(4, 2, 80, 256)

            loop(5, cols)
            for copy in swap(s):
                copy.start()

            @pl.when(s < 4)
            def _():
                def tile(t):
                    r = rows(t, TM)
                    da_v[r] += dot_bt(big[r, 0 : 2 * Q], wgu_v[at])

                loop(tokens // TM, tile)

    loop(ITEMS + 4, step)
    loop(SLOTS, lambda k: settle(ITEMS - SLOTS + k))
    oss[...] = ss_v[...]


def reduce_gradients(x, dy, wg, wu, wd):
    tokens = x.shape[0]
    hbm, vmem, dma = pl.BlockSpec(memory_space=pl.ANY), pl.BlockSpec(memory_space=pltpu.VMEM), pltpu.SemaphoreType.DMA
    return pl.pallas_call(
        step_kernel,
        name="step_kernel",
        out_shape=(
            jax.ShapeDtypeStruct((2, LAYERS, 80, F), bf16),
            jax.ShapeDtypeStruct((2, LAYERS, 80, F), bf16),
            jax.ShapeDtypeStruct((2, LAYERS, 320, D), bf16),
            jax.ShapeDtypeStruct((8, 2 * Q), f32),
        ),
        in_specs=[hbm] * 5,
        out_specs=(hbm, hbm, hbm, vmem),
        scratch_shapes=[
            pltpu.VMEM((tokens, D), bf16),
            pltpu.VMEM((2, tokens, D), bf16),
            pltpu.VMEM((tokens, D), bf16),
            pltpu.VMEM((tokens, F), bf16),
            pltpu.VMEM((tokens, D), f32),
            pltpu.VMEM((2, D, 2 * Q), bf16),
            pltpu.VMEM((2, Q, D), bf16),
            pltpu.VMEM((F, D), bf16),
            pltpu.VMEM((SLOTS, 4, 2, 80, 2 * Q), bf16),
            pltpu.VMEM((SLOTS, 2, 320, D), bf16),
            pltpu.VMEM((SLOTS, 4, 80, 2 * Q), bf16),
            pltpu.VMEM((SLOTS, 320, D), bf16),
            pltpu.VMEM((2, 2, 2, 80, 2 * Q), bf16),
            pltpu.VMEM((2, 320, D), bf16),
            pltpu.VMEM((8, 2 * Q), f32),
            dma((3,)),
            dma((2, 3)),
            dma((SLOTS, 2)),
            dma((SLOTS, 2)),
            dma((2, SLOTS, 3)),
            dma((2, 2, 3)),
            dma((SLOTS, 5)),
            pltpu.SemaphoreType.REGULAR((2,)),
            pltpu.SemaphoreType.REGULAR,
        ],
        compiler_params=pltpu.CompilerParams(collective_id=0, has_side_effects=True, vmem_limit_bytes=67043328),
    )(x, dy, wg, wu, wd)


def gather_kernel(
    ss, eg, eu, ed, wg, wu, wd, mg, mu, md, vg, vu, vd, og, ou, od, qg, qu, qd, oc,
    gg, gu, gd, bg, bu, bd, fg, fu, fd, sg, su, sd, sums, part,
    sum_send, sum_recv, g_sem, g_send, in_sem, z_send, z_recv, p_send, p_recv, q_sem,
):
    me, z, c = place()
    partner = {"dp": me + 1 - 2 * c}
    end = (z == 0) | (z == 3)
    inner = me + 2 - 4 * lax.div(z, 3)
    ends, gs, outs = (eg, eu, ed), (gg, gu, gd), (og, ou, od)

    def cut(ref, mat, half, lead, first):
        if mat < 2:
            return ref.at[(*lead, pl.ds(pl.multiple_of(first * 80, 16), 80), rows(half, 1280))]
        return ref.at[(*lead, pl.ds(pl.multiple_of(first * 320 + half * 160, 32), 160), slice(None))]

    def state(mat):
        n = 80 if mat < 2 else 320
        w = (wg, wu, wd)[mat].at[:, pl.ds(pl.multiple_of(me * n, 16), n)]
        return (
            pltpu.make_async_copy((mg, mu, md)[mat], (fg, fu, fd)[mat], in_sem.at[mat, 0]),
            pltpu.make_async_copy((vg, vu, vd)[mat], (sg, su, sd)[mat], in_sem.at[mat, 1]),
            pltpu.make_async_copy(w, (bg, bu, bd)[mat], in_sem.at[mat, 2]),
        )

    def own_g(mat):
        return pltpu.make_async_copy(ends[mat].at[0], gs[mat], q_sem.at[mat, 0])

    def keep_g(mat):
        return pltpu.make_async_copy(gs[mat], (qg, qu, qd)[mat], q_sem.at[mat, 1])

    def hand_g(k, mat):
        l, half = lax.div(k, 2), lax.rem(k, 2)
        return pltpu.make_async_remote_copy(
            cut(ends[mat], mat, half, (1, l), 0), cut(gs[mat], mat, half, (l,), 0), g_send.at[k, mat], g_sem.at[k, mat],
            device_id={"dp": inner},
        )

    def send_sum(k):
        return pltpu.make_async_remote_copy(
            part, sums.at[me], sum_send.at[k], sum_recv.at[me], device_id={"dp": lax.rem(me + k, 8)}
        )

    def get_sum(k):
        of = lax.rem(me + k, 8)
        return pltpu.make_async_remote_copy(part, sums.at[of], sum_send.at[k], sum_recv.at[of], device_id={"dp": of})

    def chunk(k, mat, block):
        l, half = lax.div(k, 2), lax.rem(k, 2)
        return cut(outs[mat], mat, half, (l,), block)

    def along(way, hop, k, mat, block):
        ref = chunk(k, mat, block)
        return pltpu.make_async_remote_copy(
            ref, ref, z_send.at[way, hop, k, mat], z_recv.at[way, hop, k, mat], device_id={"dp": me + 2 - 4 * way}
        )

    def across(k, mat, block):
        ref = chunk(k, mat, block)
        of = lax.div(block, 2)
        return pltpu.make_async_remote_copy(ref, ref, p_send.at[of, k, mat], p_recv.at[of, k, mat], device_id=partner)

    part[...] = sum(ss[:, 128 * n : 128 * n + 128] for n in range(2 * Q // 128))
    for mat in range(3):
        for copy in state(mat):
            copy.start()
    barrier = pltpu.get_barrier_semaphore()
    for k in range(1, 8):
        pl.semaphore_signal(barrier, inc=1, device_id={"dp": lax.rem(me + k, 8)})
    pl.semaphore_wait(barrier, 7)
    for k in range(1, 8):
        send_sum(k).start()

    @pl.when(end)
    def _():
        for mat in range(3):
            own_g(mat).start()

        def hand(k):
            for mat in range(3):
                hand_g(k, mat).start()

        loop(4, hand)

    sums[me] = part[...]
    for k in range(1, 8):
        get_sum(k).wait_recv()
    total = jnp.zeros((1, 1), f32)
    for k in range(8):
        total += jnp.sum(jnp.sum(sums[k], 0, keepdims=True), 1, keepdims=True)
    count = LAYERS * 3 * D * F
    factor = jnp.minimum(1.0, 0.5 * lax.rsqrt(total * (1.0 / count) + 1e-30))
    oc[...] = jnp.broadcast_to(factor, oc.shape)
    for mat in range(3):
        for copy in state(mat):
            copy.wait()

    @pl.when(end)
    def _():
        for mat in range(3):
            own_g(mat).wait()

    def adamw(k):
        l, half = lax.div(k, 2), lax.rem(k, 2)
        for mat in range(3):
            @pl.when(jnp.logical_not(end))
            def _():
                hand_g(k, mat).wait_recv()

            def piece(n):
                if mat < 2:
                    r, col = rows(n, 16), rows(half, 1280)
                    to = (l, pl.ds(pl.multiple_of(me * 80 + n * 16, 16), 16), col)
                else:
                    r, col = pl.ds(pl.multiple_of(half * 160 + n * 32, 32), 32), slice(None)
                    to = (l, pl.ds(pl.multiple_of(me * 320 + half * 160 + n * 32, 32), 32), col)
                g = gs[mat][l, r, col].astype(f32) * oc[0:1, 0:1]
                w = (bg, bu, bd)[mat][l, r, col].astype(f32)
                m = 0.9 * (fg, fu, fd)[mat][l, r, col] + 0.1 * g
                v = 0.95 * (sg, su, sd)[mat][l, r, col] + 0.05 * g * g
                outs[mat][to] = (w - 0.02 * (m * lax.rsqrt(v + 1e-8) + 0.1 * w)).astype(bf16)

            loop(5, piece)

            @pl.when(z > 0)
            def _():
                along(1, 0, k, mat, me).start()

            @pl.when(z < 3)
            def _():
                along(0, 0, k, mat, me).start()

            across(k, mat, me).start()

    loop(4, adamw)
    for mat in range(3):
        keep_g(mat).start()

    def onward(n):
        hop, k = lax.div(n, 4) + 1, lax.rem(n, 4)
        for mat in range(3):
            @pl.when(z + hop <= 3)
            def _():
                block = me + 2 * hop
                along(1, hop - 1, k, mat, block).wait_recv()

                @pl.when(z > 0)
                def _():
                    along(1, hop, k, mat, block).start()

                across(k, mat, block).start()

            @pl.when(z - hop >= 0)
            def _():
                block = me - 2 * hop
                along(0, hop - 1, k, mat, block).wait_recv()

                @pl.when(z < 3)
                def _():
                    along(0, hop, k, mat, block).start()

                across(k, mat, block).start()

    loop(12, onward)

    def finish(n):
        of, k = lax.div(n, 4), lax.rem(n, 4)
        for mat in range(3):
            across(k, mat, 2 * of + c).wait_send()
            across(k, mat, 2 * of + 1 - c).wait_recv()

            @pl.when((of >= z) & (z > 0))
            def _():
                along(1, of - z, k, mat, 2 * of + c).wait_send()

            @pl.when((of <= z) & (z < 3))
            def _():
                along(0, z - of, k, mat, 2 * of + c).wait_send()

    loop(16, finish)
    for k in range(1, 8):
        send_sum(k).wait_send()
    for mat in range(3):
        keep_g(mat).wait()

    @pl.when(end)
    def _():
        def hand(k):
            for mat in range(3):
                hand_g(k, mat).wait_send()

        loop(4, hand)


def gather_weights(ss, g, w, m, v):
    hbm, vmem, dma = pl.BlockSpec(memory_space=pl.ANY), pl.BlockSpec(memory_space=pltpu.VMEM), pltpu.SemaphoreType.DMA
    block = [(LAYERS, 80, F), (LAYERS, 80, F), (LAYERS, 320, D)]
    return pl.pallas_call(
        gather_kernel,
        name="gather_kernel",
        out_shape=(
            pltpu.VMEM((LAYERS, D, F), bf16),
            pltpu.VMEM((LAYERS, D, F), bf16),
            pltpu.VMEM((LAYERS, F, D), bf16),
            *(jax.ShapeDtypeStruct(s, bf16) for s in block),
            jax.ShapeDtypeStruct((8, 128), f32),
        ),
        in_specs=[vmem] + [hbm] * 12,
        out_specs=(vmem, vmem, vmem, hbm, hbm, hbm, vmem),
        scratch_shapes=[
            *(pltpu.VMEM(s, bf16) for s in block),
            *(pltpu.VMEM(s, bf16) for s in block),
            *(pltpu.VMEM(s, f32) for s in block),
            *(pltpu.VMEM(s, f32) for s in block),
            pltpu.VMEM((8, 8, 128), f32),
            pltpu.VMEM((8, 128), f32),
            dma((8,)),
            dma((8,)),
            dma((4, 3)),
            dma((4, 3)),
            dma((3, 3)),
            dma((2, 4, 4, 3)),
            dma((2, 4, 4, 3)),
            dma((4, 4, 3)),
            dma((4, 4, 3)),
            dma((3, 2)),
        ],
        compiler_params=pltpu.CompilerParams(collective_id=1, has_side_effects=True, vmem_limit_bytes=36 << 20),
    )(ss, *g, *w, *m, *v)


def solution(mesh):
    def body(x, dy, *arrays):
        w, m, v = arrays[0:3], arrays[3:6], arrays[6:9]
        *ends, ss = reduce_gradients(x[0], dy[0], *w)
        *rest, factor = gather_weights(ss, ends, w, m, v)
        new_w, own = rest[0:3], rest[3:6]
        c = factor[0, 0]
        g = [t.astype(f32) * c for t in own]
        new_m = [0.9 * a + 0.1 * b for a, b in zip(m, g, strict=True)]
        new_v = [0.95 * a + 0.05 * b * b for a, b in zip(v, g, strict=True)]
        return (*new_w, *new_m, *new_v)

    rep, part = P("rep", None, None), P("rep", "dp", None)
    whole, block = P(None, None, None), P(None, "dp", None)
    seq = P(("rep", "dp"), None, None)
    return jax.shard_map(
        body,
        mesh=mesh,
        in_specs=(seq, seq, *[whole] * 3, *[block] * 6),
        out_specs=(*[rep] * 3, *[part] * 6),
        check_vma=False,
    )
```

time: 822 us -> 436 us (0.53)
  waiting for transfers between devices: 466 us -> 0 us
  Pallas kernels: 0 us -> 417 us
  matrix products: 217 us -> 0 us
  other arithmetic: 65.4 us -> 6.87 us
  local copies, waits for them, and re-layouts: 32.7 us -> 11.2 us
  between operations: 17.8 us -> 0.7 us
  blocking collectives: 14.9 us -> 0 us
    pallas_call x0 -> x2, Pallas kernels: none -> 417 us  [the longest x1 243 us: reduce_gradients(): pl.pallas_call(step_kernel, name='step_kernel', out_shape=(jax.ShapeDtype...]
    unnamed x15 -> x0, waiting for transfers between devices: 276 us -> none
    dot_general x15 -> x0, matrix products: 217 us -> none  [the longest x5 77.1 us: layer(): up = jnp.dot(a, w['w_up'], preferred_element_type=jnp.float32)]
    reshape x3 -> x0, waiting for transfers between devices: 189 us -> none  [step(): t.reshape(-1, *t.shape[2:])]
    unnamed x4 -> x0, other arithmetic: 37.5 us -> none
    unnamed x43 -> x21, local copies, waits for them, and re-layouts: 32.1 us -> 9.28 us
    reshape x3 -> x0, other arithmetic: 15.2 us -> none  [step(): t.reshape(-1, *t.shape[2:])]
    reduce_sum x1 -> x0, blocking collectives: 14.9 us -> none  [of_a_group(): jnp.sum(g * g)]
  transfers between devices with their start and end apart: 9 -> 0, of which waited for: 7 -> 0; matrix products, arithmetic and copies ran while one was open for 22% -> 0% of each run, Pallas kernels for 0% -> 0%
where the time goes in v1:
time: 436 us; the launch traced here: 435 us
  Pallas kernels  417 us (96%)
  local copies, waits for them, and re-layouts  11.2 us (3%)
  other arithmetic  6.87 us (2%)
    pallas_call x1, Pallas kernels, reduce_gradients(): pl.pallas_call(step_kernel, name='step_kernel', out_shape=(jax.ShapeDtype...  243 us
    pallas_call x1, Pallas kernels, gather_weights(): pl.pallas_call(gather_kernel, name='gather_kernel', out_shape=(pltpu.VMEM...  173 us
    unnamed x21, local copies, waits for them, and re-layouts  9.28 us

profile of v1, /device:TPU:0, one launch (start us, length us, event | category | flops | bytes accessed | tf_op | source)
XLA Modules:
  0.0 435.3 jit_solution(18042958484843619796)
XLA Ops:
  0.6 243.3 %step_kernel.1 = (bf16[2,2,80,2560]{3,2,1,0:T(8,128)(2,1)}, bf16[2,2,80,2560]{3,2,1,0:T(8,128)(2,1)}, bf16[2,2,320,640]{3,2,1,0:T(8,128)(2,1)}, f32[8,1280]{1,0:T(8,128)}) custom-call(bf16[2048,640]{1,0:T(8,128)(2,1)} %bitcast.3, bf16[2048,640]{1,0:T(8,128)(2,1)} %bitcast.4, bf16[2,640,2560]{2,1,0:T(8,128)(2,1)} %wg.3, bf16[2,640,2560]{2,1,0:T(8,128)(2,1)} %wu.3, ...), custom_call_target="tpu_custom_call" | custom-call | tf_op jit(solution)/shard_map/step_kernel/pallas_call | solution.py:386
  244.0 173.2 %gather_kernel.1 = (bf16[2,640,2560]{2,1,0:T(8,128)(2,1)S(1)}, bf16[2,640,2560]{2,1,0:T(8,128)(2,1)S(1)}, bf16[2,2560,640]{2,1,0:T(8,128)(2,1)S(1)}, bf16[2,80,2...) custom-call(f32[8,1280]{1,0:T(8,128)} %get-tuple-element.20.ss, ...), custom_call_target="tpu_custom_call" | custom-call | tf_op jit(solution)/shard_map/gather_kernel/pallas_call | solution.py:624
  417.2 2.8 copy.23
  420.0 2.8 copy.24
  422.8 0.0 copy-start
  422.8 0.0 copy-start.1
  422.8 0.0 copy-start.2
  422.8 0.0 copy-start.3
  422.8 0.0 copy-start.7
  422.8 0.0 copy-start.8
  422.8 3.3 copy.25
  426.1 2.0 slice.3
  428.1 0.0 copy-done
  428.1 0.0 copy-done.1
  428.1 0.0 copy-done.2
  428.1 0.0 copy-done.3
  428.1 0.1 copy-done.7
  428.2 0.2 copy-done.8
  428.5 0.0 copy-start.4
  428.5 4.1 fusion
  432.6 0.0 copy-done.4
  432.6 0.0 copy-done.5
  432.6 0.0 copy-done.6
  432.6 2.7 fusion.2
  (2 shorter events, 0.0 us)
Async XLA Ops:
  422.8 5.3 %copy-start = (f32[2,80,2560]{2,1,0:T(8,128)S(1)}, f32[2,80,2560]{2,1,0:T(8,128)}, u32[]{:S(2)}) copy-start(f32[2,80,2560]{2,1,0:T(8,128)} %mg.1) | copy-start | bytes 4915204
  422.8 5.3 %copy-start.1 = (f32[2,80,2560]{2,1,0:T(8,128)S(1)}, f32[2,80,2560]{2,1,0:T(8,128)}, u32[]{:S(2)}) copy-start(f32[2,80,2560]{2,1,0:T(8,128)} %mu.1) | copy-start | bytes 4915204
  422.8 5.3 %copy-start.2 = (f32[2,80,2560]{2,1,0:T(8,128)S(1)}, f32[2,80,2560]{2,1,0:T(8,128)}, u32[]{:S(2)}) copy-start(f32[2,80,2560]{2,1,0:T(8,128)} %vg.1) | copy-start | bytes 4915204
  422.8 5.3 %copy-start.3 = (f32[2,80,2560]{2,1,0:T(8,128)S(1)}, f32[2,80,2560]{2,1,0:T(8,128)}, u32[]{:S(2)}) copy-start(f32[2,80,2560]{2,1,0:T(8,128)} %vu.1) | copy-start | bytes 4915204
  422.8 5.4 %copy-start.7 = (bf16[2,80,2560]{2,1,0:T(8,128)(2,1)S(1)}, bf16[2,80,2560]{2,1,0:T(8,128)(2,1)}, u32[]{:S(2)}) copy-start(bf16[2,80,2560]{2,1,0:T(8,128)(2,1)} %get-tuple-element.27) | copy-start | bytes 2457604
  422.8 5.7 %copy-start.8 = (bf16[2,80,2560]{2,1,0:T(8,128)(2,1)S(1)}, bf16[2,80,2560]{2,1,0:T(8,128)(2,1)}, u32[]{:S(2)}) copy-start(bf16[2,80,2560]{2,1,0:T(8,128)(2,1)} %get-tuple-element.29) | copy-start | bytes 2457604
  428.5 4.1 copy-start.4
  428.5 4.1 copy-start.5
  428.5 4.1 copy-start.6

commit v2 on v0

v2 whole, which is shorter than its diff:
```python
import functools

import jax
import jax.numpy as jnp
from jax import lax
from jax.experimental import pallas as pl
from jax.experimental.pallas import tpu as pltpu
from jax.sharding import PartitionSpec as P

f32, bf16 = jnp.float32, jnp.bfloat16
D, F, Q = 640, 2560, 640
LAYERS = 2
R, DROWS, DHALF = 80, 320, 160
WIDE, EVEN, EDGE = 1280, 512, 768
LANES, TILE, PACK, EIGHT = 128, 256, 16, 8
KINDS, BOTH = range(3), range(2)
HEAD = 4
LAG = 6
ITEMS = 8
SLOTS = 4
TM = 1024
COLS = ((0, TILE), (TILE, TILE), (EVEN, LANES))


def dot(a, b):
    return jnp.dot(a, b, preferred_element_type=f32)


def dot_bt(a, b):
    return lax.dot_general(a, b, (((1,), (1,)), ((), ())), preferred_element_type=f32)


def dot_at(a, b):
    return lax.dot_general(a, b, (((0,), (0,)), ((), ())), preferred_element_type=f32)


def sigmoid(g):
    return 0.5 * jnp.tanh(0.5 * g) + 0.5


def odd(i):
    return lax.rem(i, 2)


def half(i):
    return lax.div(i, 2)


def span(start, n):
    return pl.ds(pl.multiple_of(start, LANES if n % LANES == 0 else PACK), n)


def rows(t, n):
    return pl.ds(pl.multiple_of(t * n, n), n)


def loop(n, body):
    lax.fori_loop(0, n, lambda i, _: (body(i), 0)[1], 0)


def place():
    me = lax.axis_index("dp")
    return me, half(me), odd(me)


def quarter(i):
    r = lax.rem(i, 4)
    o, h = odd(r), half(r)
    return (1 - o) * (2 + h) + o * (1 - h)


def step_kernel(
    x, dy, wg, wu, wd, og, ou, od, oss, gate_h, up_h, act_h,
    h_v, a_v, dy_v, big, stage, wgu_v, wdb_v, wda_v, own, pair, got, ss_v,
    in_sem, w_sem, save_sem, psend, precv, send_sem, recv_sem, keep_sem, hsend, hrecv, credit, dcredit, pcredit,
):
    tokens = x.shape[0]
    tiles = tokens // TM
    me, z, c = place()
    partner = {"dp": me + 1 - 2 * c}

    def weights(l, q, slot, down=True):
        cols = rows(q, Q)
        first = pl.ds(pl.multiple_of(q * Q, LANES), EVEN)
        last = pl.ds(pl.multiple_of(q * Q + EVEN, LANES), LANES)
        two = (
            pltpu.make_async_copy(wg.at[l, :, cols], wgu_v.at[slot, :, 0:D], w_sem.at[slot, 0]),
            pltpu.make_async_copy(wu.at[l, :, last], wgu_v.at[slot, :, D:EDGE], w_sem.at[slot, 1]),
            pltpu.make_async_copy(wu.at[l, :, first], wgu_v.at[slot, :, EDGE:WIDE], w_sem.at[slot, 2]),
        )
        return two + (pltpu.make_async_copy(wd.at[l, cols], wdb_v.at[slot], w_sem.at[slot, 3]),) if down else two

    da_v = stage.at[0]

    def held(n, t):
        b, at = odd(t), rows(t, TM)
        return [(stage.at[b, k * TM : k * TM + TM], ref.at[n, at], save_sem.at[b, k]) for k, ref in ((0, gate_h), (1, up_h))]

    def save(n, t):
        return [pltpu.make_async_copy(here, there, sem) for here, there, sem in held(n, t)]

    def fetch(n, t):
        return [pltpu.make_async_copy(there, here, sem) for here, there, sem in held(n, t)]

    def save_act(n):
        return pltpu.make_async_copy(big.at[:, rows(n, Q)], act_h.at[n], save_sem.at[2, 0])

    def fetch_act(n):
        return pltpu.make_async_copy(act_h.at[n], big.at[:, 2 * Q : 3 * Q], save_sem.at[2, 1])

    load_x = pltpu.make_async_copy(x, h_v, in_sem.at[0])
    load_dy = pltpu.make_async_copy(dy, dy_v, in_sem.at[1])
    load_wd = pltpu.make_async_copy(wd.at[0], wda_v, in_sem.at[2])
    load_x.start()
    for copy in weights(0, 0, 0, False):
        copy.start()
    load_wd.start()
    load_dy.start()

    ss_v[...] = jnp.zeros_like(ss_v)

    def clear(k):
        for way in BOTH:
            got[way, k] = jnp.zeros((R, D), bf16)

    loop(PACK, clear)
    barrier = pltpu.get_barrier_semaphore()
    pl.semaphore_signal(barrier, device_id=partner)

    @pl.when(z > 0)
    def _():
        pl.semaphore_signal(barrier, device_id={"dp": me - 2})

    @pl.when(z < 3)
    def _():
        pl.semaphore_signal(barrier, device_id={"dp": me + 2})

    load_x.wait()

    def norm(l):
        def tile(t):
            r = rows(t, TILE)
            wide = h_v[r].astype(f32)
            a = (wide * lax.rsqrt(jnp.mean(wide * wide, -1, keepdims=True) + 1e-6)).astype(bf16)
            a_v[l, r] = a

        loop(tokens // TILE, tile)

    norm(0)

    def gate_up(a, slot):
        for c0, cn in COLS:
            if cn == TILE:
                yield c0, cn, dot(a, wgu_v[slot, :, c0 : c0 + TILE]), dot(a, wgu_v[slot, :, EDGE + c0 : 1024 + c0])
            else:
                both = dot(a, wgu_v[slot, :, EVEN:EDGE])
                yield c0, cn, both[:, 0:LANES], both[:, LANES:TILE]

    def forward(n):
        slot = odd(n)
        for copy in weights(0, n, slot, False):
            copy.wait()

        @pl.when(n < 3)
        def _():
            for copy in weights(0, n + 1, 1 - slot, False):
                copy.start()

        def tile(t):
            @pl.when((n > 0) | (t >= 2))
            def _():
                for copy in save(n, t):
                    copy.wait()

            r = rows(t, TM)
            b = odd(t)
            a = a_v[0, r]
            for c0, cn, g, u in gate_up(a, slot):
                big[r, pl.ds(pl.multiple_of(n * Q + c0, LANES), cn)] = (g * sigmoid(g) * u).astype(bf16)
                stage[b, 0:TM, c0 : c0 + cn] = g
                stage[b, TM : 2 * TM, c0 : c0 + cn] = u
            for copy in save(n, t):
                copy.start()

        loop(tiles, tile)

        @pl.when(n > 0)
        def _():
            save_act(n - 1).wait()

        save_act(n).start()

    loop(4, forward)
    for copy in weights(1, quarter(0), 0):
        copy.start()
    load_wd.wait()

    def down(t):
        r = rows(t, TM)
        h_v[r] = h_v[r] + dot(big[r], wda_v[...]).astype(bf16)

    loop(tiles, down)
    norm(1)
    for t in (tiles - 2, tiles - 1):
        for copy in save(3, t):
            copy.wait()
    save_act(3).wait()

    def zero(t):
        da_v[rows(t, LANES)] = jnp.zeros((LANES, D), f32)

    loop(tokens // LANES, zero)
    load_dy.wait()
    near = 2 + lax.convert_element_type((z > 0) & (z < 3), jnp.int32)
    pl.semaphore_wait(barrier, near)

    def is_last(way):
        return z == 3 * (1 - way)

    def is_first(way):
        return z == 3 * way

    def onward(way):
        return {"dp": me + 2 - 4 * way}

    def half_of(ref, k, h):
        return ref.at[(*k, slice(None), pl.ds(pl.multiple_of(D * h, LANES), D))]

    def send(way, item, k, h, u, g):
        slot = lax.rem(item, SLOTS)
        return pltpu.make_async_remote_copy(
            half_of(own, (slot, k, c), h), got.at[way, g], send_sem.at[way, slot, u], recv_sem.at[way, g], device_id=onward(way)
        )

    def keep(way, item, k, u, kind):
        slot, q, l = lax.rem(item, SLOTS), quarter(item), 1 - lax.div(item, 4)
        if kind == 0:
            j, p = way * q + (1 - way) * (3 - q), u - 4
            out = od.at[j, l, pl.ds(pl.multiple_of(p * R, PACK), R)]
            return [pltpu.make_async_copy(half_of(own, (slot, k, c), odd(p)), out, keep_sem.at[slot, u])]
        b = odd(u)
        j = way * b + (1 - way) * (1 - b)
        mine, out = own.at[slot, k, c], (og, ou)[kind - 1].at[j, l]
        if kind == 1:
            return [pltpu.make_async_copy(mine.at[:, 0:D], out.at[:, rows(q, Q)], keep_sem.at[slot, u])]
        first = pl.ds(pl.multiple_of(q * Q, LANES), EVEN)
        last = pl.ds(pl.multiple_of(q * Q + EVEN, LANES), LANES)
        return [
            pltpu.make_async_copy(mine.at[:, EDGE:WIDE], out.at[:, first], keep_sem.at[slot, u]),
            pltpu.make_async_copy(mine.at[:, D:EDGE], out.at[:, last], keep_sem.at[slot, 6 + u]),
        ]

    def gu_unit(way, item, u):
        return 2 * (1 - way) + odd(u), half(u), odd(item) * 4 + u

    def d_unit(item, p):
        return 4 + half(p), odd(p), EIGHT + odd(half(item)) * 4 + p

    def swap(item, kind):
        slot = lax.rem(item, SLOTS)
        if kind == 0:
            src, dst = own.at[slot, 4:6, 1 - c], pair.at[slot, 4:6]
        else:
            cols = slice(D * (kind - 1), D * kind)
            src, dst = own.at[slot, 0:4, 1 - c, :, cols], pair.at[slot, 0:4, :, cols]
        return pltpu.make_async_remote_copy(src, dst, psend.at[slot, kind], precv.at[slot, kind], device_id=partner)

    def settle(item):
        for kind in KINDS:
            swap(item, kind).wait_send()

        def one(way):
            @pl.when(is_last(way))
            def _():
                for u in range(4):
                    for copy in keep(way, item, gu_unit(way, item, u)[0], u, 1 + u // 2):
                        copy.wait()

                @pl.when(odd(item) == way)
                def _():
                    for p in range(4):
                        for copy in keep(way, item, d_unit(item, p)[0], 4 + p, 0):
                            copy.wait()

            @pl.when(jnp.logical_not(is_last(way)))
            def _():
                for u in range(4):
                    k, h, g = gu_unit(way, item, u)
                    send(way, item, k, h, u, g).wait_send()

                @pl.when(odd(item) == way)
                def _():
                    for p in range(4):
                        k, h, g = d_unit(item, p)
                        send(way, item, k, h, 4 + p, g).wait_send()

        loop(2, one)

    def unit(way, n):
        i, j = lax.div(n, 6), lax.rem(n, 6)
        late = odd(i + way)
        first, last = is_first(way), is_last(way)
        passes = jnp.logical_not(last)
        back = {"dp": me - 2 + 4 * way}

        @pl.when(passes & (i >= 2) & (j == 2))
        def _():
            pl.semaphore_wait(credit.at[way])

        @pl.when(passes & (i >= 4) & (j == 0) & (late == 0))
        def _():
            pl.semaphore_wait(dcredit.at[way])

        is_d = lax.convert_element_type(j < 2, jnp.int32)
        item = i - is_d * late
        some = lax.convert_element_type(item >= 0, jnp.int32)
        more = is_d * (1 - late) * lax.div(i, ITEMS - 1)
        v = lax.max(j - 2, 0)

        def one(x, _):
            p = 2 * late + j + 2 * x
            k, h, g = (is_d * a + (1 - is_d) * b for a, b in zip(d_unit(item, p), gu_unit(way, item, v), strict=True))
            u = is_d * (4 + p) + (1 - is_d) * v
            slot = lax.rem(item, SLOTS)
            mine, other = half_of(own, (slot, k, c), h), half_of(pair, (slot, k), h)

            @pl.when(jnp.logical_not(first))
            def _():
                send(way, item, k, h, u, g).wait_recv()

            total = (mine[...].astype(f32) + other[...].astype(f32) + got[way, g].astype(f32)).astype(bf16)
            mine[...] = total

            @pl.when(passes)
            def _():
                send(way, item, k, h, u, g).start()

            @pl.when(last)
            def _():
                wide = mine[...].astype(f32)
                ss_v[...] += jnp.sum((wide * wide).reshape(10, EIGHT, D), 0)
                for kind in KINDS:
                    @pl.when(half(j) == kind)
                    def _():
                        for copy in keep(way, item, k, u, kind):
                            copy.start()

            return 0

        lax.fori_loop(0, some * (1 + more), one, 0)

        @pl.when(jnp.logical_not(first) & (i < ITEMS - 2) & (j == 5))
        def _():
            pl.semaphore_signal(credit.at[way], device_id=back)

        @pl.when(jnp.logical_not(first) & (late == 1) & (i >= 1) & (i <= 4) & (j == 1))
        def _():
            pl.semaphore_signal(dcredit.at[way], device_id=back)

    upper = half(z)

    def engine(e):
        n = e - HEAD
        for kind in KINDS:
            @pl.when((n >= 0) & (n < 6 * ITEMS) & (lax.rem(n, 6) == 2 * kind))
            def _():
                swap(lax.div(n, 6), kind).wait_recv()

        def one(j):
            way = upper * j + (1 - upper) * (1 - j)
            hops = way * (3 - z) + (1 - way) * z
            mine = n - half(LAG * hops)

            @pl.when((mine >= 0) & (mine < 6 * ITEMS))
            def _():
                unit(way, mine)

        loop(2, one)

    def backward_norm():
        def tile(t):
            r = rows(t, TILE)
            wide, da = h_v[r].astype(f32), da_v[r].astype(bf16).astype(f32)
            scale = lax.rsqrt(jnp.mean(wide * wide, -1, keepdims=True) + 1e-6)
            dot_mean = jnp.mean(da * wide, -1, keepdims=True)
            dwide = scale * da - wide * (scale * scale * scale * dot_mean)
            dy_v[r] = (dy_v[r].astype(f32) + dwide.astype(bf16).astype(f32)).astype(bf16)

        loop(tokens // TILE, tile)

    inner = me + 2 - 4 * lax.div(z, 3)
    is_end = (z == 0) | (z == 3)

    def hand():
        return [
            pltpu.make_async_remote_copy(og.at[1, 1, :, 0:WIDE], og.at[0, 1, :, 0:WIDE], hsend.at[0], hrecv.at[0], device_id={"dp": inner}),
            pltpu.make_async_remote_copy(ou.at[1, 1, :, 0:WIDE], ou.at[0, 1, :, 0:WIDE], hsend.at[1], hrecv.at[1], device_id={"dp": inner}),
            pltpu.make_async_remote_copy(od.at[1, 1, 0:DHALF], od.at[0, 1, 0:DHALF], hsend.at[2], hrecv.at[2], device_id={"dp": inner}),
        ]

    def step(s):
        l, slot, at = 1 - lax.div(s, 4), lax.rem(s, SLOTS), odd(s)
        q, e = quarter(s), 6 * s
        for copy in weights(l, q, at):
            copy.wait()

        @pl.when(s < ITEMS - 1)
        def _():
            for copy in weights(1 - lax.div(s + 1, 4), quarter(s + 1), 1 - at):
                copy.start()

        @pl.when(s == 4)
        def _():
            backward_norm()
            for t in BOTH:
                for copy in fetch(q, t):
                    copy.start()

        def slopes(r, c0, cn, g, u, d):
            sig = sigmoid(g)
            silu = g * sig
            big[r, c0 : c0 + cn] = (d * (u * (sig + silu * (1 - sig)))).astype(bf16)
            to = EDGE + c0 if cn == TILE else D
            big[r, to : to + cn] = (d * silu).astype(bf16)
            return silu

        def tile(t):
            r = rows(t, TM)

            @pl.when(s < 4)
            def _():
                a, dh = a_v[1, r], dy_v[r]
                for c0, cn, g, u in gate_up(a, at):
                    d = dot_bt(dh, wdb_v[at, c0 : c0 + cn]).astype(bf16).astype(f32)
                    silu = slopes(r, c0, cn, g, u, d)
                    big[r, 2 * Q + c0 : 2 * Q + c0 + cn] = (silu * u).astype(bf16)

            @pl.when(s >= 4)
            def _():
                for copy in fetch(q, t):
                    copy.wait()
                b, dh = odd(t), dy_v[r]
                for c0, cn in COLS:
                    d = dot_bt(dh, wdb_v[at, c0 : c0 + cn]).astype(bf16).astype(f32)
                    slopes(r, c0, cn, stage[b, 0:TM, c0 : c0 + cn], stage[b, TM : 2 * TM, c0 : c0 + cn], d)

                @pl.when(s < ITEMS - 1)
                def _():
                    for copy in fetch(quarter(s + 1), t):
                        copy.start()

            engine(e + t)

        loop(2, tile)

        @pl.when(s >= 4)
        def _():
            fetch_act(q).wait()
            settle(s - SLOTS)
            pl.semaphore_wait(pcredit)

        once = 1 + lax.div(s, ITEMS)

        def down_part(_):
            value = dot_at(big[:, 2 * Q : 3 * Q], dy_v[...]).astype(bf16).reshape(2, 2, 2, R, D)
            for h in BOTH:
                for core in BOTH:
                    own[slot, 4:6, core, :, D * h : D * h + D] = value[core, :, h]

        loop(once, down_part)
        swap(s, 0).start()

        @pl.when((s >= 3) & (s < ITEMS - 1))
        def _():
            fetch_act(quarter(s + 1)).start()

        engine(e + 2)

        def gate_part(_):
            own[slot, 0:4, :, :, 0:EDGE] = dot_at(a_v[l], big[:, 0:EDGE]).astype(bf16).reshape(4, 2, R, EDGE)

        loop(once, gate_part)
        swap(s, 1).start()
        engine(e + 3)
        own[slot, 0:4, :, :, EDGE:WIDE] = dot_at(a_v[l], big[:, EDGE:WIDE]).astype(bf16).reshape(4, 2, R, EVEN)
        swap(s, 2).start()
        engine(e + 4)

        @pl.when(s < 4)
        def _():
            def tile(t):
                r = rows(t, TM)
                da_v[r] += dot_bt(big[r, 0 : 2 * Q], wgu_v[at])

            loop(tiles, tile)

        engine(e + 5)

        @pl.when((s >= SLOTS - 1) & (s < ITEMS - 1))
        def _():
            pl.semaphore_signal(pcredit, device_id=partner)

    loop(ITEMS, step)

    def tail(k):
        @pl.when(is_end & (k == HEAD))
        def _():
            for copy in hand():
                copy.start()

        engine(6 * ITEMS + k)

    loop(HEAD + (LAG * 3) // 2, tail)
    loop(SLOTS, lambda k: settle(ITEMS - SLOTS + k))

    @pl.when(is_end)
    def _():
        for copy in hand():
            copy.wait_send()

    @pl.when(jnp.logical_not(is_end))
    def _():
        for copy in hand():
            copy.wait_recv()

    oss[...] = ss_v[...]


def reduce_gradients(x, dy, wg, wu, wd):
    tokens = x.shape[0]
    hbm, vmem, dma = pl.BlockSpec(memory_space=pl.ANY), pl.BlockSpec(memory_space=pltpu.VMEM), pltpu.SemaphoreType.DMA
    regular = pltpu.SemaphoreType.REGULAR
    return pl.pallas_call(
        step_kernel,
        name="step_kernel",
        out_shape=(
            jax.ShapeDtypeStruct((2, LAYERS, R, F), bf16),
            jax.ShapeDtypeStruct((2, LAYERS, R, F), bf16),
            jax.ShapeDtypeStruct((2, LAYERS, DROWS, D), bf16),
            jax.ShapeDtypeStruct((EIGHT, D), f32),
            jax.ShapeDtypeStruct((4, tokens, Q), f32),
            jax.ShapeDtypeStruct((4, tokens, Q), f32),
            jax.ShapeDtypeStruct((4, tokens, Q), bf16),
        ),
        in_specs=[hbm] * 5,
        out_specs=(hbm, hbm, hbm, vmem, hbm, hbm, hbm),
        scratch_shapes=[
            pltpu.VMEM((tokens, D), bf16),
            pltpu.VMEM((2, tokens, D), bf16),
            pltpu.VMEM((tokens, D), bf16),
            pltpu.VMEM((tokens, F), bf16),
            pltpu.VMEM((2, tokens, D), f32),
            pltpu.VMEM((2, D, 2 * Q), bf16),
            pltpu.VMEM((2, Q, D), bf16),
            pltpu.VMEM((F, D), bf16),
            pltpu.VMEM((SLOTS, 6, 2, R, WIDE), bf16),
            pltpu.VMEM((SLOTS, 6, R, WIDE), bf16),
            pltpu.VMEM((2, PACK, R, D), bf16),
            pltpu.VMEM((EIGHT, D), f32),
            dma((3,)),
            dma((2, 4)),
            dma((3, 2)),
            dma((SLOTS, 3)),
            dma((SLOTS, 3)),
            dma((2, SLOTS, EIGHT)),
            dma((2, PACK)),
            dma((SLOTS, 10)),
            dma((3,)),
            dma((3,)),
            regular((2,)),
            regular((2,)),
            regular,
        ],
        compiler_params=pltpu.CompilerParams(collective_id=0, has_side_effects=True, vmem_limit_bytes=67043328),
    )(x, dy, wg, wu, wd)


def gather_kernel(
    ss, eg, eu, ed, wg, wu, wd, mg, mu, md, vg, vu, vd, og, ou, od, fg, fu, fd, sg, su, sd,
    gg, gu, gd, bg, bu, bd, sums, part, fac,
    sum_send, sum_recv, g_recv, g_send, in_sem, z_send, z_recv, p_send, p_recv, own_sem,
):
    me, z, c = place()
    partner = {"dp": me + 1 - 2 * c}
    is_end = (z == 0) | (z == 3)
    inner = me + 2 - 4 * lax.div(z, 3)
    ends, gs, outs = (eg, eu, ed), (gg, gu, gd), (og, ou, od)

    def layer_half(k):
        return 1 - half(k), odd(k)

    def cut(ref, mat, part, lead, first):
        if mat < 2:
            return ref.at[(*lead, pl.ds(pl.multiple_of(first * R, PACK), R), rows(part, WIDE))]
        return ref.at[(*lead, pl.ds(pl.multiple_of(first * DROWS + part * DHALF, 32), DHALF), slice(None))]

    def state(mat):
        n = R if mat < 2 else DROWS
        w = (wg, wu, wd)[mat].at[:, pl.ds(pl.multiple_of(me * n, PACK), n)]
        return (
            pltpu.make_async_copy((mg, mu, md)[mat], (fg, fu, fd)[mat], in_sem.at[mat, 0]),
            pltpu.make_async_copy((vg, vu, vd)[mat], (sg, su, sd)[mat], in_sem.at[mat, 1]),
            pltpu.make_async_copy(w, (bg, bu, bd)[mat], in_sem.at[mat, 2]),
        )

    def own_g(k, mat):
        l, part = layer_half(k)
        return pltpu.make_async_copy(cut(ends[mat], mat, part, (0, l), 0), cut(gs[mat], mat, part, (l,), 0), own_sem.at[k, mat])

    def hand_g(k, mat):
        l, part = layer_half(k)
        return pltpu.make_async_remote_copy(
            cut(ends[mat], mat, part, (1, l), 0), cut(gs[mat], mat, part, (l,), 0), g_send.at[k, mat], g_recv.at[k, mat],
            device_id={"dp": inner},
        )

    def send_sum(k):
        return pltpu.make_async_remote_copy(
            part, sums.at[me], sum_send.at[k], sum_recv.at[me], device_id={"dp": lax.rem(me + k, EIGHT)}
        )

    def get_sum(k):
        of = lax.rem(me + k, EIGHT)
        return pltpu.make_async_remote_copy(part, sums.at[of], sum_send.at[k], sum_recv.at[of], device_id={"dp": of})

    def chunk(k, mat, block):
        l, part = layer_half(k)
        return cut(outs[mat], mat, part, (l,), block)

    def along(way, hop, k, mat, block):
        ref = chunk(k, mat, block)
        return pltpu.make_async_remote_copy(
            ref, ref, z_send.at[way, hop, k, mat], z_recv.at[way, hop, k, mat], device_id={"dp": me + 2 - 4 * way}
        )

    def across(k, mat, block):
        ref = chunk(k, mat, block)
        of = half(block)
        return pltpu.make_async_remote_copy(ref, ref, p_send.at[of, k, mat], p_recv.at[of, k, mat], device_id=partner)

    part[...] = sum(ss[:, LANES * n : LANES * n + LANES] for n in range(5))
    sums[me] = part[...]
    barrier = pltpu.get_barrier_semaphore()
    for k in range(1, EIGHT):
        pl.semaphore_signal(barrier, device_id={"dp": lax.rem(me + k, EIGHT)})
    for mat in KINDS:
        for copy in state(mat):
            copy.start()

    def take(k):
        @pl.when(is_end | (k == 0))
        def _():
            for mat in KINDS:
                own_g(k, mat).start()

    loop(4, take)
    pl.semaphore_wait(barrier, 7)
    for k in range(1, EIGHT):
        send_sum(k).start()

    @pl.when(is_end)
    def _():
        def hand(k):
            for mat in KINDS:
                hand_g(k + 1, mat).start()

        loop(3, hand)

    for k in range(1, EIGHT):
        get_sum(k).wait_recv()
    total = jnp.zeros((EIGHT, LANES), f32)
    for k in range(EIGHT):
        total += sums[k]
    total = jnp.sum(jnp.sum(total, 0, keepdims=True), 1, keepdims=True)
    count = LAYERS * 3 * D * F
    factor = jnp.minimum(1.0, 0.5 * lax.rsqrt(total * (1.0 / count) + 1e-30))
    fac[...] = jnp.broadcast_to(factor, fac.shape)
    for mat in KINDS:
        for copy in state(mat):
            copy.wait()

    def adamw(k):
        l, part = layer_half(k)
        for mat in KINDS:
            @pl.when(is_end | (k == 0))
            def _():
                own_g(k, mat).wait()

            @pl.when(jnp.logical_not(is_end) & (k > 0))
            def _():
                hand_g(k, mat).wait_recv()

            def piece(n):
                if mat < 2:
                    r, col = rows(n, PACK), rows(part, WIDE)
                    to = (l, pl.ds(pl.multiple_of(me * R + n * PACK, PACK), PACK), col)
                else:
                    r, col = pl.ds(pl.multiple_of(part * DHALF + n * 32, 32), 32), slice(None)
                    to = (l, pl.ds(pl.multiple_of(me * DROWS + part * DHALF + n * 32, 32), 32), col)
                g = gs[mat][l, r, col].astype(f32) * fac[0:1, 0:1]
                w = (bg, bu, bd)[mat][l, r, col].astype(f32)
                m = 0.9 * (fg, fu, fd)[mat][l, r, col] + 0.1 * g
                v = 0.95 * (sg, su, sd)[mat][l, r, col] + 0.05 * g * g
                (fg, fu, fd)[mat][l, r, col] = m
                (sg, su, sd)[mat][l, r, col] = v
                outs[mat][to] = (w - 0.02 * (m * lax.rsqrt(v + 1e-8) + 0.1 * w)).astype(bf16)

            loop(5, piece)

            @pl.when(z > 0)
            def _():
                along(1, 0, k, mat, me).start()

            @pl.when(z < 3)
            def _():
                along(0, 0, k, mat, me).start()

            across(k, mat, me).start()

    loop(4, adamw)

    def onward(n):
        hop, k = lax.div(n, 4) + 1, lax.rem(n, 4)
        for mat in KINDS:
            @pl.when(z + hop <= 3)
            def _():
                block = me + 2 * hop
                along(1, hop - 1, k, mat, block).wait_recv()

                @pl.when(z > 0)
                def _():
                    along(1, hop, k, mat, block).start()

                across(k, mat, block).start()

            @pl.when(z - hop >= 0)
            def _():
                block = me - 2 * hop
                along(0, hop - 1, k, mat, block).wait_recv()

                @pl.when(z < 3)
                def _():
                    along(0, hop, k, mat, block).start()

                across(k, mat, block).start()

    loop(12, onward)

    def finish(n):
        of, k = lax.div(n, 4), lax.rem(n, 4)
        for mat in KINDS:
            across(k, mat, 2 * of + c).wait_send()
            across(k, mat, 2 * of + 1 - c).wait_recv()

            @pl.when((of >= z) & (z > 0))
            def _():
                along(1, of - z, k, mat, 2 * of + c).wait_send()

            @pl.when((of <= z) & (z < 3))
            def _():
                along(0, z - of, k, mat, 2 * of + c).wait_send()

    loop(PACK, finish)
    for k in range(1, EIGHT):
        send_sum(k).wait_send()

    @pl.when(is_end)
    def _():
        def hand(k):
            for mat in KINDS:
                hand_g(k + 1, mat).wait_send()

        loop(3, hand)


def gather_weights(ss, g, w, m, v):
    hbm, vmem, dma = pl.BlockSpec(memory_space=pl.ANY), pl.BlockSpec(memory_space=pltpu.VMEM), pltpu.SemaphoreType.DMA
    block = [(LAYERS, R, F), (LAYERS, R, F), (LAYERS, DROWS, D)]
    return pl.pallas_call(
        gather_kernel,
        name="gather_kernel",
        out_shape=(
            pltpu.VMEM((LAYERS, D, F), bf16),
            pltpu.VMEM((LAYERS, D, F), bf16),
            pltpu.VMEM((LAYERS, F, D), bf16),
            *(pltpu.VMEM(s, f32) for s in block),
            *(pltpu.VMEM(s, f32) for s in block),
        ),
        in_specs=[vmem] + [hbm] * 12,
        out_specs=(vmem,) * 9,
        scratch_shapes=[
            *(pltpu.VMEM(s, bf16) for s in block),
            *(pltpu.VMEM(s, bf16) for s in block),
            pltpu.VMEM((EIGHT, EIGHT, LANES), f32),
            pltpu.VMEM((EIGHT, LANES), f32),
            pltpu.VMEM((EIGHT, LANES), f32),
            dma((EIGHT,)),
            dma((EIGHT,)),
            dma((4, 3)),
            dma((4, 3)),
            dma((3, 3)),
            dma((2, 4, 4, 3)),
            dma((2, 4, 4, 3)),
            dma((4, 4, 3)),
            dma((4, 4, 3)),
            dma((4, 3)),
        ],
        compiler_params=pltpu.CompilerParams(collective_id=1, has_side_effects=True, vmem_limit_bytes=PACK << 20),
    )(ss, *(pltpu.with_memory_space_constraint(t, pltpu.HBM) for t in (*g, *w, *m, *v)))


def put_kernel(*refs):
    *arrays, sem = refs
    count = len(arrays) // 2
    copies = [pltpu.make_async_copy(arrays[n], arrays[count + n], sem.at[n]) for n in range(count)]
    for copy in copies:
        copy.start()
    for copy in copies:
        copy.wait()


def put(arrays):
    any_space = pl.BlockSpec(memory_space=pl.ANY)
    arrays = [pltpu.with_memory_space_constraint(a, pltpu.VMEM) for a in arrays]
    return pl.pallas_call(
        put_kernel,
        name="put_kernel",
        out_shape=tuple(pltpu.HBM(a.shape, a.dtype) for a in arrays),
        in_specs=[any_space] * len(arrays),
        out_specs=(any_space,) * len(arrays),
        scratch_shapes=[pltpu.SemaphoreType.DMA((len(arrays),))],
        compiler_params=pltpu.CompilerParams(vmem_limit_bytes=1 << 20),
    )(*arrays)


def solution(mesh):
    def body(x, dy, *arrays):
        w, m, v = arrays[0:3], arrays[3:6], arrays[6:9]
        *ends, ss = reduce_gradients(x[0], dy[0], *w)[0:4]
        return put(gather_weights(ss, ends, w, m, v))

    rep, part = P("rep", None, None), P("rep", "dp", None)
    whole, block = P(None, None, None), P(None, "dp", None)
    seq = P(("rep", "dp"), None, None)
    return jax.shard_map(
        body,
        mesh=mesh,
        in_specs=(seq, seq, *[whole] * 3, *[block] * 6),
        out_specs=(*[rep] * 3, *[part] * 6),
        check_vma=False,
    )
```

time: 822 us -> 383 us (0.47)
  waiting for transfers between devices: 466 us -> 0 us
  Pallas kernels: 0 us -> 381 us
  matrix products: 217 us -> 0 us
  other arithmetic: 65.4 us -> 0 us
  local copies, waits for them, and re-layouts: 32.7 us -> 0.72 us
  between operations: 17.8 us -> 0.83 us
  blocking collectives: 14.9 us -> 0 us
    pallas_call x0 -> x3, Pallas kernels: none -> 381 us  [the longest x1 201 us: reduce_gradients(): pl.pallas_call(step_kernel, name='step_kernel', out_shape=(jax.ShapeDtype...]
    unnamed x15 -> x0, waiting for transfers between devices: 276 us -> none
    dot_general x15 -> x0, matrix products: 217 us -> none  [the longest x5 77.1 us: layer(): up = jnp.dot(a, w['w_up'], preferred_element_type=jnp.float32)]
    reshape x3 -> x0, waiting for transfers between devices: 189 us -> none  [step(): t.reshape(-1, *t.shape[2:])]
    unnamed x4 -> x0, other arithmetic: 37.5 us -> none
    unnamed x43 -> x2, local copies, waits for them, and re-layouts: 32.1 us -> 0.72 us
    reshape x3 -> x0, other arithmetic: 15.2 us -> none  [step(): t.reshape(-1, *t.shape[2:])]
    reduce_sum x1 -> x0, blocking collectives: 14.9 us -> none  [of_a_group(): jnp.sum(g * g)]
  transfers between devices with their start and end apart: 9 -> 0, of which waited for: 7 -> 0; matrix products, arithmetic and copies ran while one was open for 22% -> 0% of each run, Pallas kernels for 0% -> 0%
where the time goes in v2:
time: 383 us; the launch traced here: 382 us
  Pallas kernels  381 us (99%)
    pallas_call x1, Pallas kernels, reduce_gradients(): pl.pallas_call(step_kernel, name='step_kernel', out_shape=(jax.ShapeDtype...  201 us
    pallas_call x1, Pallas kernels, gather_weights(): pl.pallas_call(gather_kernel, name='gather_kernel', out_shape=(pltpu.VMEM...  170 us
    pallas_call x1, Pallas kernels, put(): pl.pallas_call(put_kernel, name='put_kernel', out_shape=tuple((pltpu.HBM(...  9.81 us

profile of v2, /device:TPU:0, one launch (start us, length us, event | category | flops | bytes accessed | tf_op | source)
XLA Modules:
  0.0 382.4 jit_solution(6501034221332975006)
XLA Ops:
  0.6 201.1 %step_kernel.1 = (bf16[2,2,80,2560]{3,2,1,0:T(8,128)(2,1)}, bf16[2,2,80,2560]{3,2,1,0:T(8,128)(2,1)}, bf16[2,2,320,640]{3,2,1,0:T(8,128)(2,1)}, f32[8,640]{1,0:T...) custom-call(bf16[2048,640]{1,0:T(8,128)(2,1)} %bitcast.2, ...), custom_call_target="tpu_custom_call" | custom-call | tf_op jit(solution)/shard_map/step_kernel/pallas_call | solution.py:533
  201.7 0.0 copy-start
  201.7 0.7 copy-done
  202.4 170.0 %gather_kernel.1 = (bf16[2,640,2560]{2,1,0:T(8,128)(2,1)S(1)}, bf16[2,640,2560]{2,1,0:T(8,128)(2,1)S(1)}, bf16[2,2560,640]{2,1,0:T(8,128)(2,1)S(1)}, f32[2,80,25...) custom-call(f32[8,640]{1,0:T(8,128)S(1)} %copy-done, ...), custom_call_target="tpu_custom_call" | custom-call | tf_op jit(solution)/shard_map/gather_kernel/pallas_call | solution.py:779
  372.4 9.8 %put_kernel.1 = (bf16[2,640,2560]{2,1,0:T(8,128)(2,1)}, bf16[2,640,2560]{2,1,0:T(8,128)(2,1)}, bf16[2,2560,640]{2,1,0:T(8,128)(2,1)}, f32[2,80,2560]{2,1,0:T(8,1...) custom-call(bf16[2,640,2560]{2,1,0:T(8,128)(2,1)S(1)} %get-tuple-ele, ...), custom_call_target="tpu_custom_call" | custom-call | tf_op jit(solution)/shard_map/put_kernel/pallas_call | solution.py:825
Async XLA Ops:
  201.7 0.7 copy-start

commit v3 on v2

--- a/solution.py
+++ b/solution.py
@@ -14,7 +14,9 @@
 WIDE, EVEN, EDGE = 1280, 512, 768
 LANES, TILE, PACK, EIGHT = 128, 256, 16, 8
 KINDS, BOTH = range(3), range(2)
-HEAD = 4
+OTHERS = range(1, EIGHT)
+CHUNK = ((R, WIDE), (R, WIDE), (DHALF, D))
+HEAD = 3
 LAG = 6
 ITEMS = 8
 SLOTS = 4
@@ -38,6 +40,10 @@
     return 0.5 * jnp.tanh(0.5 * g) + 0.5
 
 
+def flip(way):
+    return 1 - way
+
+
 def odd(i):
     return lax.rem(i, 2)
 
@@ -70,9 +76,10 @@
 
 
 def step_kernel(
-    x, dy, wg, wu, wd, og, ou, od, oss, gate_h, up_h, act_h,
-    h_v, a_v, dy_v, big, stage, wgu_v, wdb_v, wda_v, own, pair, got, ss_v,
-    in_sem, w_sem, save_sem, psend, precv, send_sem, recv_sem, keep_sem, hsend, hrecv, credit, dcredit, pcredit,
+    x, dy, wg, wu, wd, mg, mu, md, vg, vu, vd,
+    og, ou, od, ofac, gate_h, up_h, act_h, emg, emu, emd, evg, evu, evd,
+    h_v, a_v, dy_v, big, stage, wgu_v, wdb_v, wda_v, own, pair, got, ss_v, sums, part,
+    in_sem, w_sem, save_sem, psend, precv, send_sem, recv_sem, keep_sem, hsend, hrecv, esend, erecv, sum_send, sum_recv, credit, dcredit, pcredit,
 ):
     tokens = x.shape[0]
     tiles = tokens // TM
@@ -125,15 +132,17 @@
 
     loop(PACK, clear)
     barrier = pltpu.get_barrier_semaphore()
-    pl.semaphore_signal(barrier, device_id=partner)
-
-    @pl.when(z > 0)
-    def _():
-        pl.semaphore_signal(barrier, device_id={"dp": me - 2})
-
-    @pl.when(z < 3)
-    def _():
-        pl.semaphore_signal(barrier, device_id={"dp": me + 2})
+    for k in OTHERS:
+        pl.semaphore_signal(barrier, device_id={"dp": lax.rem(me + k, EIGHT)})
+    is_end = (z == 0) | (z == 3)
+    is_inner = jnp.logical_not(is_end)
+
+    def early():
+        out = []
+        for n, (src, dst) in enumerate(zip((mg, mu, md, vg, vu, vd), (emg, emu, emd, evg, evu, evd), strict=True)):
+            src = src.at[0, DHALF:DROWS] if n % 3 == 2 else src.at[0, :, WIDE:F]
+            out.append(pltpu.make_async_remote_copy(src, dst, esend.at[n], erecv.at[n], device_id={"dp": me + 4 * z - 6}))
+        return out
 
     load_x.wait()
 
@@ -165,6 +174,15 @@
         def _():
             for copy in weights(0, n + 1, 1 - slot, False):
                 copy.start()
+
+        @pl.when(n == 1)
+        def _():
+            pl.semaphore_wait(barrier, EIGHT - 1)
+
+            @pl.when(is_inner)
+            def _():
+                for copy in early():
+                    copy.start()
 
         def tile(t):
             @pl.when((n > 0) | (t >= 2))
@@ -211,11 +229,11 @@
 
     loop(tokens // LANES, zero)
     load_dy.wait()
-    near = 2 + lax.convert_element_type((z > 0) & (z < 3), jnp.int32)
-    pl.semaphore_wait(barrier, near)
+    for copy in fetch(quarter(4), 1):
+        copy.start()
 
     def is_last(way):
-        return z == 3 * (1 - way)
+        return z == 3 * flip(way)
 
     def is_first(way):
         return z == 3 * way
@@ -235,11 +253,11 @@
     def keep(way, item, k, u, kind):
         slot, q, l = lax.rem(item, SLOTS), quarter(item), 1 - lax.div(item, 4)
         if kind == 0:
-            j, p = way * q + (1 - way) * (3 - q), u - 4
+            j, p = way * q + flip(way) * (3 - q), u - 4
             out = od.at[j, l, pl.ds(pl.multiple_of(p * R, PACK), R)]
             return [pltpu.make_async_copy(half_of(own, (slot, k, c), odd(p)), out, keep_sem.at[slot, u])]
         b = odd(u)
-        j = way * b + (1 - way) * (1 - b)
+        j = way * b + flip(way) * (1 - b)
         mine, out = own.at[slot, k, c], (og, ou)[kind - 1].at[j, l]
         if kind == 1:
             return [pltpu.make_async_copy(mine.at[:, 0:D], out.at[:, rows(q, Q)], keep_sem.at[slot, u])]
@@ -251,7 +269,7 @@
         ]
 
     def gu_unit(way, item, u):
-        return 2 * (1 - way) + odd(u), half(u), odd(item) * 4 + u
+        return 2 * flip(way) + odd(u), half(u), odd(item) * 4 + u
 
     def d_unit(item, p):
         return 4 + half(p), odd(p), EIGHT + odd(half(item)) * 4 + p
@@ -368,7 +386,7 @@
 
         def one(j):
             way = upper * j + (1 - upper) * (1 - j)
-            hops = way * (3 - z) + (1 - way) * z
+            hops = way * (3 - z) + flip(way) * z
             mine = n - half(LAG * hops)
 
             @pl.when((mine >= 0) & (mine < 6 * ITEMS))
@@ -389,8 +407,6 @@
         loop(tokens // TILE, tile)
 
     inner = me + 2 - 4 * lax.div(z, 3)
-    is_end = (z == 0) | (z == 3)
-
     def hand():
         return [
             pltpu.make_async_remote_copy(og.at[1, 1, :, 0:WIDE], og.at[0, 1, :, 0:WIDE], hsend.at[0], hrecv.at[0], device_id={"dp": inner}),
@@ -412,9 +428,8 @@
         @pl.when(s == 4)
         def _():
             backward_norm()
-            for t in BOTH:
-                for copy in fetch(q, t):
-                    copy.start()
+            for copy in fetch(q, 0):
+                copy.start()
 
         def slopes(r, c0, cn, g, u, d):
             sig = sigmoid(g)
@@ -424,7 +439,8 @@
             big[r, to : to + cn] = (d * silu).astype(bf16)
             return silu
 
-        def tile(t):
+        def tile(turn):
+            t = 1 - turn
             r = rows(t, TM)
 
             @pl.when(s < 4)
@@ -449,7 +465,7 @@
                     for copy in fetch(quarter(s + 1), t):
                         copy.start()
 
-            engine(e + t)
+            engine(e + turn)
 
         loop(2, tile)
 
@@ -511,22 +527,43 @@
         engine(6 * ITEMS + k)
 
     loop(HEAD + (LAG * 3) // 2, tail)
+
+    def exchange(k, of):
+        return pltpu.make_async_remote_copy(
+            part, sums.at[of], sum_send.at[k], sum_recv.at[of], device_id={"dp": lax.rem(me + k, EIGHT)}
+        )
+
+    part[...] = sum(ss_v[:, LANES * n : LANES * n + LANES] for n in range(5))
+    for k in OTHERS:
+        exchange(k, me).start()
+    sums[me] = part[...]
     loop(SLOTS, lambda k: settle(ITEMS - SLOTS + k))
+    for k in OTHERS:
+        exchange(k, lax.rem(me + k, EIGHT)).wait_recv()
+    total = sum(sums[k] for k in range(EIGHT))
+    total = jnp.sum(jnp.sum(total, 0, keepdims=True), 1, keepdims=True)
+    count = LAYERS * 3 * D * F
+    ofac[...] = jnp.broadcast_to(jnp.minimum(1.0, 0.5 * lax.rsqrt(total * (1.0 / count) + 1e-30)), ofac.shape)
 
     @pl.when(is_end)
     def _():
         for copy in hand():
             copy.wait_send()
-
-    @pl.when(jnp.logical_not(is_end))
+        for copy in early():
+            copy.wait_recv()
+
+    @pl.when(is_inner)
     def _():
         for copy in hand():
             copy.wait_recv()
-
-    oss[...] = ss_v[...]
-
-
-def reduce_gradients(x, dy, wg, wu, wd):
+        for copy in early():
+            copy.wait_send()
+
+    for k in OTHERS:
+        exchange(k, me).wait_send()
+
+
+def reduce_gradients(x, dy, w, m, v):
     tokens = x.shape[0]
     hbm, vmem, dma = pl.BlockSpec(memory_space=pl.ANY), pl.BlockSpec(memory_space=pltpu.VMEM), pltpu.SemaphoreType.DMA
     regular = pltpu.SemaphoreType.REGULAR
@@ -534,16 +571,15 @@
         step_kernel,
         name="step_kernel",
         out_shape=(
-            jax.ShapeDtypeStruct((2, LAYERS, R, F), bf16),
-            jax.ShapeDtypeStruct((2, LAYERS, R, F), bf16),
+            *[jax.ShapeDtypeStruct((2, LAYERS, R, F), bf16)] * 2,
             jax.ShapeDtypeStruct((2, LAYERS, DROWS, D), bf16),
-            jax.ShapeDtypeStruct((EIGHT, D), f32),
-            jax.ShapeDtypeStruct((4, tokens, Q), f32),
-            jax.ShapeDtypeStruct((4, tokens, Q), f32),
+            jax.ShapeDtypeStruct((EIGHT, LANES), f32),
+            *[jax.ShapeDtypeStruct((4, tokens, Q), f32)] * 2,
             jax.ShapeDtypeStruct((4, tokens, Q), bf16),
+            *(jax.ShapeDtypeStruct(t, f32) for t in CHUNK + CHUNK),
         ),
-        in_specs=[hbm] * 5,
-        out_specs=(hbm, hbm, hbm, vmem, hbm, hbm, hbm),
+        in_specs=[hbm] * 11,
+        out_specs=(hbm, hbm, hbm, vmem, *[hbm] * 9),
         scratch_shapes=[
             pltpu.VMEM((tokens, D), bf16),
             pltpu.VMEM((2, tokens, D), bf16),
@@ -557,6 +593,8 @@
             pltpu.VMEM((SLOTS, 6, R, WIDE), bf16),
             pltpu.VMEM((2, PACK, R, D), bf16),
             pltpu.VMEM((EIGHT, D), f32),
+            pltpu.VMEM((EIGHT, EIGHT, LANES), f32),
+            pltpu.VMEM((EIGHT, LANES), f32),
             dma((3,)),
             dma((2, 4)),
             dma((3, 2)),
@@ -565,20 +603,19 @@
             dma((2, SLOTS, EIGHT)),
             dma((2, PACK)),
             dma((SLOTS, 10)),
-            dma((3,)),
-            dma((3,)),
+            *[dma((EIGHT,))] * 6,
             regular((2,)),
             regular((2,)),
             regular,
         ],
         compiler_params=pltpu.CompilerParams(collective_id=0, has_side_effects=True, vmem_limit_bytes=67043328),
-    )(x, dy, wg, wu, wd)
+    )(x, dy, *w, *m, *v)
 
 
 def gather_kernel(
-    ss, eg, eu, ed, wg, wu, wd, mg, mu, md, vg, vu, vd, og, ou, od, fg, fu, fd, sg, su, sd,
-    gg, gu, gd, bg, bu, bd, sums, part, fac,
-    sum_send, sum_recv, g_recv, g_send, in_sem, z_send, z_recv, p_send, p_recv, own_sem,
+    ofac, emg, emu, emd, evg, evu, evd, eg, eu, ed, wg, wu, wd, mg, mu, md, vg, vu, vd, og, ou, od, fg, fu, fd, sg, su, sd,
+    gg, gu, gd, bg, bu, bd, xmg, xmu, xmd, xvg, xvu, xvd, xgg, xgu, xgd, xwg, xwu, xwd, fac,
+    fac_sem, x_sem, g_recv, g_send, in_sem, z_send, z_recv, p_send, p_recv, own_sem,
 ):
     me, z, c = place()
     partner = {"dp": me + 1 - 2 * c}
@@ -594,14 +631,14 @@
             return ref.at[(*lead, pl.ds(pl.multiple_of(first * R, PACK), R), rows(part, WIDE))]
         return ref.at[(*lead, pl.ds(pl.multiple_of(first * DROWS + part * DHALF, 32), DHALF), slice(None))]
 
-    def state(mat):
+    def state(mat, l):
         n = R if mat < 2 else DROWS
-        w = (wg, wu, wd)[mat].at[:, pl.ds(pl.multiple_of(me * n, PACK), n)]
-        return (
-            pltpu.make_async_copy((mg, mu, md)[mat], (fg, fu, fd)[mat], in_sem.at[mat, 0]),
-            pltpu.make_async_copy((vg, vu, vd)[mat], (sg, su, sd)[mat], in_sem.at[mat, 1]),
-            pltpu.make_async_copy(w, (bg, bu, bd)[mat], in_sem.at[mat, 2]),
-        )
+        w = (wg, wu, wd)[mat].at[l, pl.ds(pl.multiple_of(me * n, PACK), n)]
+        sources = ((mg, mu, md)[mat].at[l], (vg, vu, vd)[mat].at[l], w)
+        return [
+            pltpu.make_async_copy(src, there[mat].at[l], in_sem.at[mat, l, n])
+            for n, (src, there) in enumerate(zip(sources, ((fg, fu, fd), (sg, su, sd), (bg, bu, bd)), strict=True))
+        ]
 
     def own_g(k, mat):
         l, part = layer_half(k)
@@ -614,14 +651,14 @@
             device_id={"dp": inner},
         )
 
-    def send_sum(k):
-        return pltpu.make_async_remote_copy(
-            part, sums.at[me], sum_send.at[k], sum_recv.at[me], device_id={"dp": lax.rem(me + k, EIGHT)}
+    def outer(mat):
+        w = (wg, wu, wd)[mat]
+        return (
+            pltpu.make_async_copy((emg, emu, emd)[mat], (xmg, xmu, xmd)[mat], x_sem.at[mat, 0]),
+            pltpu.make_async_copy((evg, evu, evd)[mat], (xvg, xvu, xvd)[mat], x_sem.at[mat, 1]),
+            pltpu.make_async_copy(cut(ends[mat], mat, 1, (1, 0), 0), (xgg, xgu, xgd)[mat], x_sem.at[mat, 2]),
+            pltpu.make_async_copy(cut(w, mat, 1, (0,), inner), (xwg, xwu, xwd)[mat], x_sem.at[mat, 3]),
         )
-
-    def get_sum(k):
-        of = lax.rem(me + k, EIGHT)
-        return pltpu.make_async_remote_copy(part, sums.at[of], sum_send.at[k], sum_recv.at[of], device_id={"dp": of})
 
     def chunk(k, mat, block):
         l, part = layer_half(k)
@@ -638,14 +675,24 @@
         of = half(block)
         return pltpu.make_async_remote_copy(ref, ref, p_send.at[of, k, mat], p_recv.at[of, k, mat], device_id=partner)
 
-    part[...] = sum(ss[:, LANES * n : LANES * n + LANES] for n in range(5))
-    sums[me] = part[...]
     barrier = pltpu.get_barrier_semaphore()
-    for k in range(1, EIGHT):
-        pl.semaphore_signal(barrier, device_id={"dp": lax.rem(me + k, EIGHT)})
-    for mat in KINDS:
-        for copy in state(mat):
-            copy.start()
+    pl.semaphore_signal(barrier, device_id=partner)
+
+    @pl.when(z > 0)
+    def _():
+        pl.semaphore_signal(barrier, device_id={"dp": me - 2})
+
+    @pl.when(z < 3)
+    def _():
+        pl.semaphore_signal(barrier, device_id={"dp": me + 2})
+
+    factor = pltpu.make_async_copy(ofac, fac, fac_sem)
+    factor.start()
+
+    def load(l):
+        for mat in KINDS:
+            for copy in state(mat, l):
+                copy.start()
 
     def take(k):
         @pl.when(is_end | (k == 0))
@@ -653,35 +700,45 @@
             for mat in KINDS:
                 own_g(k, mat).start()
 
-    loop(4, take)
-    pl.semaphore_wait(barrier, 7)
-    for k in range(1, EIGHT):
-        send_sum(k).start()
+    take(0)
+    load(1)
+    pl.semaphore_wait(barrier, 2 + lax.convert_element_type(jnp.logical_not(is_end), jnp.int32))
 
     @pl.when(is_end)
     def _():
+        for mat in KINDS:
+            for copy in outer(mat):
+                copy.start()
+
         def hand(k):
             for mat in KINDS:
                 hand_g(k + 1, mat).start()
 
         loop(3, hand)
 
-    for k in range(1, EIGHT):
-        get_sum(k).wait_recv()
-    total = jnp.zeros((EIGHT, LANES), f32)
-    for k in range(EIGHT):
-        total += sums[k]
-    total = jnp.sum(jnp.sum(total, 0, keepdims=True), 1, keepdims=True)
-    count = LAYERS * 3 * D * F
-    factor = jnp.minimum(1.0, 0.5 * lax.rsqrt(total * (1.0 / count) + 1e-30))
-    fac[...] = jnp.broadcast_to(factor, fac.shape)
-    for mat in KINDS:
-        for copy in state(mat):
-            copy.wait()
+    load(0)
+    loop(3, lambda k: take(k + 1))
+    factor.wait()
+
+    def stepped(g, w, m, v):
+        g = g.astype(f32) * fac[0:1, 0:1]
+        w = w.astype(f32)
+        m = 0.9 * m + 0.1 * g
+        v = 0.95 * v + 0.05 * g * g
+        return m, v, (w - 0.02 * (m * lax.rsqrt(v + 1e-8) + 0.1 * w)).astype(bf16)
+
+    def crosses(way, k):
+        edge, near = 3 * flip(way), 2 - way
+        return (z != edge) & ((z != near) | (k < 3))
 
     def adamw(k):
         l, part = layer_half(k)
         for mat in KINDS:
+            @pl.when(part == 0)
+            def _():
+                for copy in state(mat, l):
+                    copy.wait()
+
             @pl.when(is_end | (k == 0))
             def _():
                 own_g(k, mat).wait()
@@ -697,32 +754,50 @@
                 else:
                     r, col = pl.ds(pl.multiple_of(part * DHALF + n * 32, 32), 32), slice(None)
                     to = (l, pl.ds(pl.multiple_of(me * DROWS + part * DHALF + n * 32, 32), 32), col)
-                g = gs[mat][l, r, col].astype(f32) * fac[0:1, 0:1]
-                w = (bg, bu, bd)[mat][l, r, col].astype(f32)
-                m = 0.9 * (fg, fu, fd)[mat][l, r, col] + 0.1 * g
-                v = 0.95 * (sg, su, sd)[mat][l, r, col] + 0.05 * g * g
+                m, v, w = stepped(
+                    gs[mat][l, r, col], (bg, bu, bd)[mat][l, r, col], (fg, fu, fd)[mat][l, r, col], (sg, su, sd)[mat][l, r, col]
+                )
                 (fg, fu, fd)[mat][l, r, col] = m
                 (sg, su, sd)[mat][l, r, col] = v
-                outs[mat][to] = (w - 0.02 * (m * lax.rsqrt(v + 1e-8) + 0.1 * w)).astype(bf16)
+                outs[mat][to] = w
 
             loop(5, piece)
 
-            @pl.when(z > 0)
-            def _():
-                along(1, 0, k, mat, me).start()
-
-            @pl.when(z < 3)
-            def _():
-                along(0, 0, k, mat, me).start()
+            for way in (1, 0):
+                @pl.when(crosses(way, k))
+                def _():
+                    along(way, 0, k, mat, me).start()
 
             across(k, mat, me).start()
 
     loop(4, adamw)
+
+    @pl.when(is_end)
+    def _():
+        for mat in KINDS:
+            for copy in outer(mat):
+                copy.wait()
+
+            def piece(n):
+                size = PACK if mat < 2 else 2 * PACK
+                r = rows(n, size)
+                new = stepped((xgg, xgu, xgd)[mat][r], (xwg, xwu, xwd)[mat][r], (xmg, xmu, xmd)[mat][r], (xvg, xvu, xvd)[mat][r])
+                if mat < 2:
+                    first, col = inner * R + n * size, slice(WIDE, F)
+                else:
+                    first, col = inner * DROWS + DHALF + n * size, slice(None)
+                outs[mat][0, pl.ds(pl.multiple_of(first, PACK), size), col] = new[2]
+
+            loop(5, piece)
+            across(3, mat, inner).start()
+
 
     def onward(n):
         hop, k = lax.div(n, 4) + 1, lax.rem(n, 4)
         for mat in KINDS:
-            @pl.when(z + hop <= 3)
+            known = (n == 3) & is_end
+
+            @pl.when((z + hop <= 3) & jnp.logical_not(known))
             def _():
                 block = me + 2 * hop
                 along(1, hop - 1, k, mat, block).wait_recv()
@@ -733,7 +808,7 @@
 
                 across(k, mat, block).start()
 
-            @pl.when(z - hop >= 0)
+            @pl.when((z - hop >= 0) & jnp.logical_not(known))
             def _():
                 block = me - 2 * hop
                 along(0, hop - 1, k, mat, block).wait_recv()
@@ -752,18 +827,15 @@
             across(k, mat, 2 * of + c).wait_send()
             across(k, mat, 2 * of + 1 - c).wait_recv()
 
-            @pl.when((of >= z) & (z > 0))
+            @pl.when((of > z) & (z > 0) | (of == z) & crosses(1, k))
             def _():
                 along(1, of - z, k, mat, 2 * of + c).wait_send()
 
-            @pl.when((of <= z) & (z < 3))
+            @pl.when((of < z) & (z < 3) | (of == z) & crosses(0, k))
             def _():
                 along(0, z - of, k, mat, 2 * of + c).wait_send()
 
     loop(PACK, finish)
-    for k in range(1, EIGHT):
-        send_sum(k).wait_send()
-
     @pl.when(is_end)
     def _():
         def hand(k):
@@ -773,7 +845,7 @@
         loop(3, hand)
 
 
-def gather_weights(ss, g, w, m, v):
+def gather_weights(factor, outer, g, w, m, v):
     hbm, vmem, dma = pl.BlockSpec(memory_space=pl.ANY), pl.BlockSpec(memory_space=pltpu.VMEM), pltpu.SemaphoreType.DMA
     block = [(LAYERS, R, F), (LAYERS, R, F), (LAYERS, DROWS, D)]
     return pl.pallas_call(
@@ -786,27 +858,25 @@
             *(pltpu.VMEM(s, f32) for s in block),
             *(pltpu.VMEM(s, f32) for s in block),
         ),
-        in_specs=[vmem] + [hbm] * 12,
+        in_specs=[hbm] * 19,
         out_specs=(vmem,) * 9,
         scratch_shapes=[
             *(pltpu.VMEM(s, bf16) for s in block),
             *(pltpu.VMEM(s, bf16) for s in block),
-            pltpu.VMEM((EIGHT, EIGHT, LANES), f32),
+            *(pltpu.VMEM(s, f32) for s in CHUNK + CHUNK),
+            *(pltpu.VMEM(s, bf16) for s in CHUNK + CHUNK),
             pltpu.VMEM((EIGHT, LANES), f32),
-            pltpu.VMEM((EIGHT, LANES), f32),
-            dma((EIGHT,)),
-            dma((EIGHT,)),
+            dma,
+            dma((3, 4)),
             dma((4, 3)),
             dma((4, 3)),
-            dma((3, 3)),
-            dma((2, 4, 4, 3)),
-            dma((2, 4, 4, 3)),
-            dma((4, 4, 3)),
-            dma((4, 4, 3)),
+            dma((3, LAYERS, 3)),
+            *[dma((2, 4, 4, 3))] * 2,
+            *[dma((4, 4, 3))] * 2,
             dma((4, 3)),
         ],
-        compiler_params=pltpu.CompilerParams(collective_id=1, has_side_effects=True, vmem_limit_bytes=PACK << 20),
-    )(ss, *(pltpu.with_memory_space_constraint(t, pltpu.HBM) for t in (*g, *w, *m, *v)))
+        compiler_params=pltpu.CompilerParams(collective_id=1, has_side_effects=True, vmem_limit_bytes=24 << 20),
+    )(*(pltpu.with_memory_space_constraint(t, pltpu.HBM) for t in (factor, *outer, *g, *w, *m, *v)))
 
 
 def put_kernel(*refs):
@@ -836,8 +906,8 @@
 def solution(mesh):
     def body(x, dy, *arrays):
         w, m, v = arrays[0:3], arrays[3:6], arrays[6:9]
-        *ends, ss = reduce_gradients(x[0], dy[0], *w)[0:4]
-        return put(gather_weights(ss, ends, w, m, v))
+        *ends, factor, _, _, _, a, b, c, d, e, f = reduce_gradients(x[0], dy[0], w, m, v)
+        return put(gather_weights(factor, (a, b, c, d, e, f), ends, w, m, v))
 
     rep, part = P("rep", None, None), P("rep", "dp", None)
     whole, block = P(None, None, None), P(None, "dp", None)

time: 383 us -> 367 us (0.958)
  Pallas kernels: 381 us -> 364 us
    pallas_call x1, Pallas kernels: 170 us -> 155 us  [gather_weights(): pl.pallas_call(gather_kernel, name='gather_kernel', out_shape=(pltpu.VMEM...]
where the time goes in v3:
time: 367 us; the launch traced here: 365 us
  Pallas kernels  364 us (99%)
    pallas_call x1, Pallas kernels, reduce_gradients(): pl.pallas_call(step_kernel, name='step_kernel', out_shape=(*[jax.ShapeDty...  200 us
    pallas_call x1, Pallas kernels, gather_weights(): pl.pallas_call(gather_kernel, name='gather_kernel', out_shape=(pltpu.VMEM...  155 us
    pallas_call x1, Pallas kernels, put(): pl.pallas_call(put_kernel, name='put_kernel', out_shape=tuple((pltpu.HBM(...  9.81 us

profile of v3, /device:TPU:0, one launch (start us, length us, event | category | flops | bytes accessed | tf_op | source)
XLA Modules:
  0.0 364.8 jit_solution(7266459389244219656)
XLA Ops:
  0.6 199.6 %step_kernel.1 = (bf16[2,2,80,2560]{3,2,1,0:T(8,128)(2,1)}, bf16[2,2,80,2560]{3,2,1,0:T(8,128)(2,1)}, bf16[2,2,320,640]{3,2,1,0:T(8,128)(2,1)}, f32[8,128]{1,0:T...) custom-call(bf16[2048,640]{1,0:T(8,128)(2,1)} %bitcast.2, ...), custom_call_target="tpu_custom_call" | custom-call | tf_op jit(solution)/shard_map/step_kernel/pallas_call | solution.py:570
  200.2 154.6 %gather_kernel.1 = (bf16[2,640,2560]{2,1,0:T(8,128)(2,1)S(1)}, bf16[2,640,2560]{2,1,0:T(8,128)(2,1)S(1)}, bf16[2,2560,640]{2,1,0:T(8,128)(2,1)S(1)}, f32[2,80,25...) custom-call(f32[8,128]{1,0:T(8,128)} %get-tuple-element.28.ofac, ...), custom_call_target="tpu_custom_call" | custom-call | tf_op jit(solution)/shard_map/gather_kernel/pallas_call | solution.py:851
  354.8 9.8 %put_kernel.1 = (bf16[2,640,2560]{2,1,0:T(8,128)(2,1)}, bf16[2,640,2560]{2,1,0:T(8,128)(2,1)}, bf16[2,2560,640]{2,1,0:T(8,128)(2,1)}, f32[2,80,2560]{2,1,0:T(8,1...) custom-call(bf16[2,640,2560]{2,1,0:T(8,128)(2,1)S(1)} %get-tuple-ele, ...), custom_call_target="tpu_custom_call" | custom-call | tf_op jit(solution)/shard_map/put_kernel/pallas_call | solution.py:895

commit v4 on v3

--- a/solution.py
+++ b/solution.py
@@ -17,7 +17,7 @@
 OTHERS = range(1, EIGHT)
 CHUNK = ((R, WIDE), (R, WIDE), (DHALF, D))
 HEAD = 3
-LAG = 6
+LAG = 3
 ITEMS = 8
 SLOTS = 4
 TM = 1024
@@ -66,7 +66,20 @@
 
 def place():
     me = lax.axis_index("dp")
-    return me, half(me), odd(me)
+    c = odd(me)
+    return me, half(me), c, {"dp": me + 1 - 2 * c}
+
+
+def ahead(me, way):
+    return {"dp": me + 2 - 4 * way}
+
+
+def at_end(z):
+    return (z == 0) | (z == 3)
+
+
+def layer_of(item):
+    return 1 - lax.div(item, 4)
 
 
 def quarter(i):
@@ -77,14 +90,13 @@
 
 def step_kernel(
     x, dy, wg, wu, wd, mg, mu, md, vg, vu, vd,
-    og, ou, od, ofac, gate_h, up_h, act_h, emg, emu, emd, evg, evu, evd,
+    og, ou, od, ofac, gate_h, up_h, act_h, emg, emu, emd, evg, evu, evd, ehm, ehv,
     h_v, a_v, dy_v, big, stage, wgu_v, wdb_v, wda_v, own, pair, got, ss_v, sums, part,
     in_sem, w_sem, save_sem, psend, precv, send_sem, recv_sem, keep_sem, hsend, hrecv, esend, erecv, sum_send, sum_recv, credit, dcredit, pcredit,
 ):
     tokens = x.shape[0]
     tiles = tokens // TM
-    me, z, c = place()
-    partner = {"dp": me + 1 - 2 * c}
+    me, z, c, partner = place()
 
     def weights(l, q, slot, down=True):
         cols = rows(q, Q)
@@ -134,15 +146,21 @@
     barrier = pltpu.get_barrier_semaphore()
     for k in OTHERS:
         pl.semaphore_signal(barrier, device_id={"dp": lax.rem(me + k, EIGHT)})
-    is_end = (z == 0) | (z == 3)
+    is_end = at_end(z)
     is_inner = jnp.logical_not(is_end)
 
-    def early():
-        out = []
-        for n, (src, dst) in enumerate(zip((mg, mu, md, vg, vu, vd), (emg, emu, emd, evg, evu, evd), strict=True)):
-            src = src.at[0, DHALF:DROWS] if n % 3 == 2 else src.at[0, :, WIDE:F]
-            out.append(pltpu.make_async_remote_copy(src, dst, esend.at[n], erecv.at[n], device_id={"dp": me + 4 * z - 6}))
-        return out
+    def early(n, src, dst):
+        return pltpu.make_async_remote_copy(src, dst, esend.at[n], erecv.at[n], device_id=ahead(me, 2 - z))
+
+    def early_chunks():
+        return [
+            early(n, src.at[0, DHALF:DROWS] if n % 3 == 2 else src.at[0, :, WIDE:F], dst)
+            for n, (src, dst) in enumerate(zip((mg, mu, md, vg, vu, vd), (emg, emu, emd, evg, evu, evd), strict=True))
+        ]
+
+    def early_piece(n, moment):
+        at = (rows(half(n), R // 2), rows(odd(n), D))
+        return early(6 + 2 * n + moment, (mg, vg)[moment].at[(0, *at)], (ehm, ehv)[moment].at[at])
 
     load_x.wait()
 
@@ -156,6 +174,12 @@
         loop(tokens // TILE, tile)
 
     norm(0)
+    pl.semaphore_wait(barrier, EIGHT - 1)
+
+    @pl.when(is_inner)
+    def _():
+        for copy in early_chunks():
+            copy.start()
 
     def gate_up(a, slot):
         for c0, cn in COLS:
@@ -174,15 +198,6 @@
         def _():
             for copy in weights(0, n + 1, 1 - slot, False):
                 copy.start()
-
-        @pl.when(n == 1)
-        def _():
-            pl.semaphore_wait(barrier, EIGHT - 1)
-
-            @pl.when(is_inner)
-            def _():
-                for copy in early():
-                    copy.start()
 
         def tile(t):
             @pl.when((n > 0) | (t >= 2))
@@ -238,20 +253,17 @@
     def is_first(way):
         return z == 3 * way
 
-    def onward(way):
-        return {"dp": me + 2 - 4 * way}
-
     def half_of(ref, k, h):
         return ref.at[(*k, slice(None), pl.ds(pl.multiple_of(D * h, LANES), D))]
 
     def send(way, item, k, h, u, g):
         slot = lax.rem(item, SLOTS)
         return pltpu.make_async_remote_copy(
-            half_of(own, (slot, k, c), h), got.at[way, g], send_sem.at[way, slot, u], recv_sem.at[way, g], device_id=onward(way)
+            half_of(own, (slot, k, c), h), got.at[way, g], send_sem.at[way, slot, u], recv_sem.at[way, g], device_id=ahead(me, way)
         )
 
     def keep(way, item, k, u, kind):
-        slot, q, l = lax.rem(item, SLOTS), quarter(item), 1 - lax.div(item, 4)
+        slot, q, l = lax.rem(item, SLOTS), quarter(item), layer_of(item)
         if kind == 0:
             j, p = way * q + flip(way) * (3 - q), u - 4
             out = od.at[j, l, pl.ds(pl.multiple_of(p * R, PACK), R)]
@@ -319,7 +331,7 @@
         late = odd(i + way)
         first, last = is_first(way), is_last(way)
         passes = jnp.logical_not(last)
-        back = {"dp": me - 2 + 4 * way}
+        back = ahead(me, flip(way))
 
         @pl.when(passes & (i >= 2) & (j == 2))
         def _():
@@ -387,7 +399,7 @@
         def one(j):
             way = upper * j + (1 - upper) * (1 - j)
             hops = way * (3 - z) + flip(way) * z
-            mine = n - half(LAG * hops)
+            mine = n - LAG * hops
 
             @pl.when((mine >= 0) & (mine < 6 * ITEMS))
             def _():
@@ -406,23 +418,24 @@
 
         loop(tokens // TILE, tile)
 
-    inner = me + 2 - 4 * lax.div(z, 3)
+    inner = ahead(me, lax.div(z, 3))
     def hand():
         return [
-            pltpu.make_async_remote_copy(og.at[1, 1, :, 0:WIDE], og.at[0, 1, :, 0:WIDE], hsend.at[0], hrecv.at[0], device_id={"dp": inner}),
-            pltpu.make_async_remote_copy(ou.at[1, 1, :, 0:WIDE], ou.at[0, 1, :, 0:WIDE], hsend.at[1], hrecv.at[1], device_id={"dp": inner}),
-            pltpu.make_async_remote_copy(od.at[1, 1, 0:DHALF], od.at[0, 1, 0:DHALF], hsend.at[2], hrecv.at[2], device_id={"dp": inner}),
+            pltpu.make_async_remote_copy(og.at[1, 1, :, 0:WIDE], og.at[0, 1, :, 0:WIDE], hsend.at[0], hrecv.at[0], device_id=inner),
+            pltpu.make_async_remote_copy(ou.at[1, 1, :, 0:WIDE], ou.at[0, 1, :, 0:WIDE], hsend.at[1], hrecv.at[1], device_id=inner),
+            pltpu.make_async_remote_copy(od.at[1, 1, 0:DHALF], od.at[0, 1, 0:DHALF], hsend.at[2], hrecv.at[2], device_id=inner),
         ]
 
     def step(s):
-        l, slot, at = 1 - lax.div(s, 4), lax.rem(s, SLOTS), odd(s)
+        l, slot, at = layer_of(s), lax.rem(s, SLOTS), odd(s)
         q, e = quarter(s), 6 * s
+        top = s < 4
         for copy in weights(l, q, at):
             copy.wait()
 
         @pl.when(s < ITEMS - 1)
         def _():
-            for copy in weights(1 - lax.div(s + 1, 4), quarter(s + 1), 1 - at):
+            for copy in weights(layer_of(s + 1), quarter(s + 1), 1 - at):
                 copy.start()
 
         @pl.when(s == 4)
@@ -443,7 +456,7 @@
             t = 1 - turn
             r = rows(t, TM)
 
-            @pl.when(s < 4)
+            @pl.when(top)
             def _():
                 a, dh = a_v[1, r], dy_v[r]
                 for c0, cn, g, u in gate_up(a, at):
@@ -451,7 +464,7 @@
                     silu = slopes(r, c0, cn, g, u, d)
                     big[r, 2 * Q + c0 : 2 * Q + c0 + cn] = (silu * u).astype(bf16)
 
-            @pl.when(s >= 4)
+            @pl.when(jnp.logical_not(top))
             def _():
                 for copy in fetch(q, t):
                     copy.wait()
@@ -465,11 +478,16 @@
                     for copy in fetch(quarter(s + 1), t):
                         copy.start()
 
+            for moment in BOTH:
+                @pl.when(top & is_inner & (turn == moment))
+                def _():
+                    early_piece(s, moment).start()
+
             engine(e + turn)
 
         loop(2, tile)
 
-        @pl.when(s >= 4)
+        @pl.when(jnp.logical_not(top))
         def _():
             fetch_act(q).wait()
             settle(s - SLOTS)
@@ -502,7 +520,7 @@
         swap(s, 2).start()
         engine(e + 4)
 
-        @pl.when(s < 4)
+        @pl.when(top)
         def _():
             def tile(t):
                 r = rows(t, TM)
@@ -526,7 +544,7 @@
 
         engine(6 * ITEMS + k)
 
-    loop(HEAD + (LAG * 3) // 2, tail)
+    loop(HEAD + 3 * LAG, tail)
 
     def exchange(k, of):
         return pltpu.make_async_remote_copy(
@@ -549,15 +567,21 @@
     def _():
         for copy in hand():
             copy.wait_send()
-        for copy in early():
+        for copy in early_chunks():
             copy.wait_recv()
+        for n in range(4):
+            for moment in BOTH:
+                early_piece(n, moment).wait_recv()
 
     @pl.when(is_inner)
     def _():
         for copy in hand():
             copy.wait_recv()
-        for copy in early():
+        for copy in early_chunks():
             copy.wait_send()
+        for n in range(4):
+            for moment in BOTH:
+                early_piece(n, moment).wait_send()
 
     for k in OTHERS:
         exchange(k, me).wait_send()
@@ -576,10 +600,10 @@
             jax.ShapeDtypeStruct((EIGHT, LANES), f32),
             *[jax.ShapeDtypeStruct((4, tokens, Q), f32)] * 2,
             jax.ShapeDtypeStruct((4, tokens, Q), bf16),
-            *(jax.ShapeDtypeStruct(t, f32) for t in CHUNK + CHUNK),
+            *(jax.ShapeDtypeStruct(t, f32) for t in (*CHUNK, *CHUNK, *CHUNK[0:2])),
         ),
         in_specs=[hbm] * 11,
-        out_specs=(hbm, hbm, hbm, vmem, *[hbm] * 9),
+        out_specs=(hbm, hbm, hbm, vmem, *[hbm] * 11),
         scratch_shapes=[
             pltpu.VMEM((tokens, D), bf16),
             pltpu.VMEM((2, tokens, D), bf16),
@@ -603,7 +627,7 @@
             dma((2, SLOTS, EIGHT)),
             dma((2, PACK)),
             dma((SLOTS, 10)),
-            *[dma((EIGHT,))] * 6,
+            *[dma((PACK,))] * 6,
             regular((2,)),
             regular((2,)),
             regular,
@@ -613,15 +637,16 @@
 
 
 def gather_kernel(
-    ofac, emg, emu, emd, evg, evu, evd, eg, eu, ed, wg, wu, wd, mg, mu, md, vg, vu, vd, og, ou, od, fg, fu, fd, sg, su, sd,
-    gg, gu, gd, bg, bu, bd, xmg, xmu, xmd, xvg, xvu, xvd, xgg, xgu, xgd, xwg, xwu, xwd, fac,
+    ofac, emg, emu, emd, evg, evu, evd, ehm, ehv, eg, eu, ed, wg, wu, wd, mg, mu, md, vg, vu, vd, og, ou, od, fg, fu, fd, sg, su, sd,
+    gg, gu, gd, bg, bu, bd, xmg, xmu, xmd, xmh, xvg, xvu, xvd, xvh, xgg, xgu, xgd, xgh, xwg, xwu, xwd, xwh, fac,
     fac_sem, x_sem, g_recv, g_send, in_sem, z_send, z_recv, p_send, p_recv, own_sem,
 ):
-    me, z, c = place()
-    partner = {"dp": me + 1 - 2 * c}
-    is_end = (z == 0) | (z == 3)
-    inner = me + 2 - 4 * lax.div(z, 3)
+    me, z, c, partner = place()
+    is_end = at_end(z)
+    inner = ahead(me, lax.div(z, 3))
+    known = 2, 3, 3
     ends, gs, outs = (eg, eu, ed), (gg, gu, gd), (og, ou, od)
+    given = (xmg, xmu, xmd, xmh), (xvg, xvu, xvd, xvh), (xgg, xgu, xgd, xgh), (xwg, xwu, xwd, xwh)
 
     def layer_half(k):
         return 1 - half(k), odd(k)
@@ -648,17 +673,18 @@
         l, part = layer_half(k)
         return pltpu.make_async_remote_copy(
             cut(ends[mat], mat, part, (1, l), 0), cut(gs[mat], mat, part, (l,), 0), g_send.at[k, mat], g_recv.at[k, mat],
-            device_id={"dp": inner},
+            device_id=inner,
         )
 
-    def outer(mat):
-        w = (wg, wu, wd)[mat]
-        return (
-            pltpu.make_async_copy((emg, emu, emd)[mat], (xmg, xmu, xmd)[mat], x_sem.at[mat, 0]),
-            pltpu.make_async_copy((evg, evu, evd)[mat], (xvg, xvu, xvd)[mat], x_sem.at[mat, 1]),
-            pltpu.make_async_copy(cut(ends[mat], mat, 1, (1, 0), 0), (xgg, xgu, xgd)[mat], x_sem.at[mat, 2]),
-            pltpu.make_async_copy(cut(w, mat, 1, (0,), inner), (xwg, xwu, xwd)[mat], x_sem.at[mat, 3]),
+    def outer(x):
+        mat, part = (x, 1) if x < 3 else (0, 0)
+        sources = (
+            (emg, emu, emd, ehm)[x],
+            (evg, evu, evd, ehv)[x],
+            cut(ends[mat], mat, part, (1, 0), 0),
+            cut((wg, wu, wd)[mat], mat, part, (0,), inner["dp"]),
         )
+        return [pltpu.make_async_copy(src, there[x], x_sem.at[x, n]) for n, (src, there) in enumerate(zip(sources, given, strict=True))]
 
     def chunk(k, mat, block):
         l, part = layer_half(k)
@@ -667,7 +693,7 @@
     def along(way, hop, k, mat, block):
         ref = chunk(k, mat, block)
         return pltpu.make_async_remote_copy(
-            ref, ref, z_send.at[way, hop, k, mat], z_recv.at[way, hop, k, mat], device_id={"dp": me + 2 - 4 * way}
+            ref, ref, z_send.at[way, hop, k, mat], z_recv.at[way, hop, k, mat], device_id=ahead(me, way)
         )
 
     def across(k, mat, block):
@@ -678,13 +704,10 @@
     barrier = pltpu.get_barrier_semaphore()
     pl.semaphore_signal(barrier, device_id=partner)
 
-    @pl.when(z > 0)
-    def _():
-        pl.semaphore_signal(barrier, device_id={"dp": me - 2})
-
-    @pl.when(z < 3)
-    def _():
-        pl.semaphore_signal(barrier, device_id={"dp": me + 2})
+    for way in BOTH:
+        @pl.when(z != 3 * flip(way))
+        def _():
+            pl.semaphore_signal(barrier, device_id=ahead(me, way))
 
     factor = pltpu.make_async_copy(ofac, fac, fac_sem)
     factor.start()
@@ -702,12 +725,14 @@
 
     take(0)
     load(1)
+    load(0)
+    loop(3, lambda k: take(k + 1))
     pl.semaphore_wait(barrier, 2 + lax.convert_element_type(jnp.logical_not(is_end), jnp.int32))
 
     @pl.when(is_end)
     def _():
-        for mat in KINDS:
-            for copy in outer(mat):
+        for x in range(4):
+            for copy in outer(x):
                 copy.start()
 
         def hand(k):
@@ -716,8 +741,6 @@
 
         loop(3, hand)
 
-    load(0)
-    loop(3, lambda k: take(k + 1))
     factor.wait()
 
     def stepped(g, w, m, v):
@@ -727,13 +750,33 @@
         v = 0.95 * v + 0.05 * g * g
         return m, v, (w - 0.02 * (m * lax.rsqrt(v + 1e-8) + 0.1 * w)).astype(bf16)
 
-    def crosses(way, k):
+    def crosses(way, k, mat):
         edge, near = 3 * flip(way), 2 - way
-        return (z != edge) & ((z != near) | (k < 3))
+        return (z != edge) & ((z != near) | (k < known[mat]))
+
+    upper = half(z)
+
+    def relay(turn, m, mat):
+        way = upper * turn + flip(upper) * flip(turn)
+        hop, k = lax.div(m, 4) + 1, lax.rem(m, 4)
+        of = z + hop * (2 * way - 1)
+        block = 2 * of + c
+
+        @pl.when((m >= 0) & (m < 12) & (of >= 0) & (of < 4) & ((m >= 4) | (m < known[mat]) | jnp.logical_not(is_end)))
+        def _():
+            along(way, hop - 1, k, mat, block).wait_recv()
+
+            @pl.when(z != 3 * flip(way))
+            def _():
+                along(way, hop, k, mat, block).start()
+
+            across(k, mat, block).start()
 
     def adamw(k):
         l, part = layer_half(k)
         for mat in KINDS:
+            relay(0, k - 2, mat)
+
             @pl.when(part == 0)
             def _():
                 for copy in state(mat, l):
@@ -764,7 +807,7 @@
             loop(5, piece)
 
             for way in (1, 0):
-                @pl.when(crosses(way, k))
+                @pl.when(crosses(way, k, mat))
                 def _():
                     along(way, 0, k, mat, me).start()
 
@@ -774,52 +817,27 @@
 
     @pl.when(is_end)
     def _():
-        for mat in KINDS:
-            for copy in outer(mat):
+        for x in range(4):
+            for copy in outer(x):
                 copy.wait()
+            mat, part = (x, 1) if x < 3 else (0, 0)
 
             def piece(n):
                 size = PACK if mat < 2 else 2 * PACK
                 r = rows(n, size)
-                new = stepped((xgg, xgu, xgd)[mat][r], (xwg, xwu, xwd)[mat][r], (xmg, xmu, xmd)[mat][r], (xvg, xvu, xvd)[mat][r])
-                if mat < 2:
-                    first, col = inner * R + n * size, slice(WIDE, F)
-                else:
-                    first, col = inner * DROWS + DHALF + n * size, slice(None)
-                outs[mat][0, pl.ds(pl.multiple_of(first, PACK), size), col] = new[2]
+                m, v, g, w = (ref[x][r] for ref in given)
+                first = inner["dp"] * (R if mat < 2 else DROWS) + n * size + (0 if mat < 2 else DHALF)
+                col = slice(WIDE * part, WIDE * part + WIDE) if mat < 2 else slice(None)
+                outs[mat][0, pl.ds(pl.multiple_of(first, PACK), size), col] = stepped(g, w, m, v)[2]
 
             loop(5, piece)
-            across(3, mat, inner).start()
-
+            across(2 + part, mat, inner["dp"]).start()
 
     def onward(n):
-        hop, k = lax.div(n, 4) + 1, lax.rem(n, 4)
         for mat in KINDS:
-            known = (n == 3) & is_end
-
-            @pl.when((z + hop <= 3) & jnp.logical_not(known))
-            def _():
-                block = me + 2 * hop
-                along(1, hop - 1, k, mat, block).wait_recv()
-
-                @pl.when(z > 0)
-                def _():
-                    along(1, hop, k, mat, block).start()
-
-                across(k, mat, block).start()
-
-            @pl.when((z - hop >= 0) & jnp.logical_not(known))
-            def _():
-                block = me - 2 * hop
-                along(0, hop - 1, k, mat, block).wait_recv()
-
-                @pl.when(z < 3)
-                def _():
-                    along(0, hop, k, mat, block).start()
-
-                across(k, mat, block).start()
-
-    loop(12, onward)
+            loop(2, lambda turn: relay(turn, n + 2 - 3 * turn, mat))
+
+    loop(13, onward)
 
     def finish(n):
         of, k = lax.div(n, 4), lax.rem(n, 4)
@@ -827,11 +845,11 @@
             across(k, mat, 2 * of + c).wait_send()
             across(k, mat, 2 * of + 1 - c).wait_recv()
 
-            @pl.when((of > z) & (z > 0) | (of == z) & crosses(1, k))
+            @pl.when((of > z) & (z > 0) | (of == z) & crosses(1, k, mat))
             def _():
                 along(1, of - z, k, mat, 2 * of + c).wait_send()
 
-            @pl.when((of < z) & (z < 3) | (of == z) & crosses(0, k))
+            @pl.when((of < z) & (z < 3) | (of == z) & crosses(0, k, mat))
             def _():
                 along(0, z - of, k, mat, 2 * of + c).wait_send()
 
@@ -858,16 +876,15 @@
             *(pltpu.VMEM(s, f32) for s in block),
             *(pltpu.VMEM(s, f32) for s in block),
         ),
-        in_specs=[hbm] * 19,
+        in_specs=[hbm] * 21,
         out_specs=(vmem,) * 9,
         scratch_shapes=[
             *(pltpu.VMEM(s, bf16) for s in block),
             *(pltpu.VMEM(s, bf16) for s in block),
-            *(pltpu.VMEM(s, f32) for s in CHUNK + CHUNK),
-            *(pltpu.VMEM(s, bf16) for s in CHUNK + CHUNK),
+            *(pltpu.VMEM(s, t) for t in (f32, f32, bf16, bf16) for s in (*CHUNK, CHUNK[0])),
             pltpu.VMEM((EIGHT, LANES), f32),
             dma,
-            dma((3, 4)),
+            dma((4, 4)),
             dma((4, 3)),
             dma((4, 3)),
             dma((3, LAYERS, 3)),
@@ -882,7 +899,7 @@
 def put_kernel(*refs):
     *arrays, sem = refs
     count = len(arrays) // 2
-    copies = [pltpu.make_async_copy(arrays[n], arrays[count + n], sem.at[n]) for n in range(count)]
+    copies = [pltpu.make_async_copy(arrays[n].at[l], arrays[count + n].at[l], sem.at[n, l]) for n in range(count) for l in range(LAYERS)]
     for copy in copies:
         copy.start()
     for copy in copies:
@@ -898,7 +915,7 @@
         out_shape=tuple(pltpu.HBM(a.shape, a.dtype) for a in arrays),
         in_specs=[any_space] * len(arrays),
         out_specs=(any_space,) * len(arrays),
-        scratch_shapes=[pltpu.SemaphoreType.DMA((len(arrays),))],
+        scratch_shapes=[pltpu.SemaphoreType.DMA((len(arrays), LAYERS))],
         compiler_params=pltpu.CompilerParams(vmem_limit_bytes=1 << 20),
     )(*arrays)
 
@@ -906,8 +923,8 @@
 def solution(mesh):
     def body(x, dy, *arrays):
         w, m, v = arrays[0:3], arrays[3:6], arrays[6:9]
-        *ends, factor, _, _, _, a, b, c, d, e, f = reduce_gradients(x[0], dy[0], w, m, v)
-        return put(gather_weights(factor, (a, b, c, d, e, f), ends, w, m, v))
+        results = reduce_gradients(x[0], dy[0], w, m, v)
+        return put(gather_weights(results[3], results[7:], results[0:3], w, m, v))
 
     rep, part = P("rep", None, None), P("rep", "dp", None)
     whole, block = P(None, None, None), P(None, "dp", None)

time: 367 us -> 363 us (0.989)
  no operation moved by 1% of the time
where the time goes in v4:
time: 363 us
  Pallas kernels  362 us (100%)
    pallas_call x1, Pallas kernels, reduce_gradients(): pl.pallas_call(step_kernel, name='step_kernel', out_shape=(*[jax.ShapeDty...  200 us
    pallas_call x1, Pallas kernels, gather_weights(): pl.pallas_call(gather_kernel, name='gather_kernel', out_shape=(pltpu.VMEM...  152 us
    pallas_call x1, Pallas kernels, put(): pl.pallas_call(put_kernel, name='put_kernel', out_shape=tuple((pltpu.HBM(...  9.87 us

profile of v4, /device:TPU:0, one launch (start us, length us, event | category | flops | bytes accessed | tf_op | source)
XLA Modules:
  0.0 363.0 jit_solution(5857525995668225241)
XLA Ops:
  0.6 200.1 %step_kernel.1 = (bf16[2,2,80,2560]{3,2,1,0:T(8,128)(2,1)}, bf16[2,2,80,2560]{3,2,1,0:T(8,128)(2,1)}, bf16[2,2,320,640]{3,2,1,0:T(8,128)(2,1)}, f32[8,128]{1,0:T...) custom-call(bf16[2048,640]{1,0:T(8,128)(2,1)} %bitcast.2, ...), custom_call_target="tpu_custom_call" | custom-call | tf_op jit(solution)/shard_map/step_kernel/pallas_call | solution.py:594
  200.7 152.2 %gather_kernel.1 = (bf16[2,640,2560]{2,1,0:T(8,128)(2,1)S(1)}, bf16[2,640,2560]{2,1,0:T(8,128)(2,1)S(1)}, bf16[2,2560,640]{2,1,0:T(8,128)(2,1)S(1)}, f32[2,80,25...) custom-call(f32[8,128]{1,0:T(8,128)} %get-tuple-element.30.ofac, ...), custom_call_target="tpu_custom_call" | custom-call | tf_op jit(solution)/shard_map/gather_kernel/pallas_call | solution.py:869
  352.9 9.9 %put_kernel.1 = (bf16[2,640,2560]{2,1,0:T(8,128)(2,1)}, bf16[2,640,2560]{2,1,0:T(8,128)(2,1)}, bf16[2,2560,640]{2,1,0:T(8,128)(2,1)}, f32[2,80,2560]{2,1,0:T(8,1...) custom-call(bf16[2,640,2560]{2,1,0:T(8,128)(2,1)S(1)} %get-tuple-ele, ...), custom_call_target="tpu_custom_call" | custom-call | tf_op jit(solution)/shard_map/put_kernel/pallas_call | solution.py:912

commit v5 on v4

--- a/solution.py
+++ b/solution.py
@@ -78,6 +78,10 @@
     return (z == 0) | (z == 3)
 
 
+def split(n):
+    return lax.div(n, 4), lax.rem(n, 4)
+
+
 def layer_of(item):
     return 1 - lax.div(item, 4)
 
@@ -127,10 +131,11 @@
     def fetch_act(n):
         return pltpu.make_async_copy(act_h.at[n], big.at[:, 2 * Q : 3 * Q], save_sem.at[2, 1])
 
-    load_x = pltpu.make_async_copy(x, h_v, in_sem.at[0])
+    load_x = [pltpu.make_async_copy(x.at[rows(n, TM)], h_v.at[rows(n, TM)], in_sem.at[2 + n]) for n in BOTH]
     load_dy = pltpu.make_async_copy(dy, dy_v, in_sem.at[1])
-    load_wd = pltpu.make_async_copy(wd.at[0], wda_v, in_sem.at[2])
-    load_x.start()
+    load_wd = pltpu.make_async_copy(wd.at[0], wda_v, in_sem.at[0])
+    for copy in load_x:
+        copy.start()
     for copy in weights(0, 0, 0, False):
         copy.start()
     load_wd.start()
@@ -162,18 +167,17 @@
         at = (rows(half(n), R // 2), rows(odd(n), D))
         return early(6 + 2 * n + moment, (mg, vg)[moment].at[(0, *at)], (ehm, ehv)[moment].at[at])
 
-    load_x.wait()
-
-    def norm(l):
+    def norm(l, n):
         def tile(t):
-            r = rows(t, TILE)
+            r = rows(n * (TM // TILE) + t, TILE)
             wide = h_v[r].astype(f32)
-            a = (wide * lax.rsqrt(jnp.mean(wide * wide, -1, keepdims=True) + 1e-6)).astype(bf16)
-            a_v[l, r] = a
-
-        loop(tokens // TILE, tile)
-
-    norm(0)
+            a_v[l, r] = (wide * lax.rsqrt(jnp.mean(wide * wide, -1, keepdims=True) + 1e-6)).astype(bf16)
+
+        loop(TM // TILE, tile)
+
+    for n, copy in enumerate(load_x):
+        copy.wait()
+        norm(0, n)
     pl.semaphore_wait(barrier, EIGHT - 1)
 
     @pl.when(is_inner)
@@ -233,7 +237,7 @@
         h_v[r] = h_v[r] + dot(big[r], wda_v[...]).astype(bf16)
 
     loop(tiles, down)
-    norm(1)
+    loop(2, lambda n: norm(1, n))
     for t in (tiles - 2, tiles - 1):
         for copy in save(3, t):
             copy.wait()
@@ -551,7 +555,7 @@
             part, sums.at[of], sum_send.at[k], sum_recv.at[of], device_id={"dp": lax.rem(me + k, EIGHT)}
         )
 
-    part[...] = sum(ss_v[:, LANES * n : LANES * n + LANES] for n in range(5))
+    part[...] = sum(ss_v[:, LANES * n : LANES * n + LANES] for n in range(D // LANES))
     for k in OTHERS:
         exchange(k, me).start()
     sums[me] = part[...]
@@ -619,7 +623,7 @@
             pltpu.VMEM((EIGHT, D), f32),
             pltpu.VMEM((EIGHT, EIGHT, LANES), f32),
             pltpu.VMEM((EIGHT, LANES), f32),
-            dma((3,)),
+            dma((4,)),
             dma((2, 4)),
             dma((3, 2)),
             dma((SLOTS, 3)),
@@ -758,7 +762,8 @@
 
     def relay(turn, m, mat):
         way = upper * turn + flip(upper) * flip(turn)
-        hop, k = lax.div(m, 4) + 1, lax.rem(m, 4)
+        hop, k = split(m)
+        hop = hop + 1
         of = z + hop * (2 * way - 1)
         block = 2 * of + c
 
@@ -833,14 +838,13 @@
             loop(5, piece)
             across(2 + part, mat, inner["dp"]).start()
 
+    far = 3 - z
+
     def onward(n):
         for mat in KINDS:
             loop(2, lambda turn: relay(turn, n + 2 - 3 * turn, mat))
 
-    loop(13, onward)
-
-    def finish(n):
-        of, k = lax.div(n, 4), lax.rem(n, 4)
+    def done(of, k):
         for mat in KINDS:
             across(k, mat, 2 * of + c).wait_send()
             across(k, mat, 2 * of + 1 - c).wait_recv()
@@ -853,7 +857,19 @@
             def _():
                 along(0, z - of, k, mat, 2 * of + c).wait_send()
 
-    loop(PACK, finish)
+    def finish(n, early):
+        of, k = split(n)
+
+        @pl.when(is_end & (of != far) if early else jnp.logical_not(is_end) | (of == far))
+        def _():
+            done(of, k)
+
+    most = 9
+    loop(most, onward)
+    loop(PACK, lambda n: finish(n, True))
+    loop(4, lambda n: onward(n + most))
+    loop(PACK, lambda n: finish(n, False))
+
     @pl.when(is_end)
     def _():
         def hand(k):

time: 363 us -> 363 us (level)
  no operation moved by 1% of the time
where the time goes in v5:
time: 363 us
  Pallas kernels  362 us (100%)
    pallas_call x1, Pallas kernels, reduce_gradients(): pl.pallas_call(step_kernel, name='step_kernel', out_shape=(*[jax.ShapeDty...  200 us
    pallas_call x1, Pallas kernels, gather_weights(): pl.pallas_call(gather_kernel, name='gather_kernel', out_shape=(pltpu.VMEM...  153 us
    pallas_call x1, Pallas kernels, put(): pl.pallas_call(put_kernel, name='put_kernel', out_shape=tuple((pltpu.HBM(...  9.87 us

profile of v5, /device:TPU:0, one launch (start us, length us, event | category | flops | bytes accessed | tf_op | source)
XLA Modules:
  0.0 363.0 jit_solution(17055310118938939915)
XLA Ops:
  0.6 199.6 %step_kernel.1 = (bf16[2,2,80,2560]{3,2,1,0:T(8,128)(2,1)}, bf16[2,2,80,2560]{3,2,1,0:T(8,128)(2,1)}, bf16[2,2,320,640]{3,2,1,0:T(8,128)(2,1)}, f32[8,128]{1,0:T...) custom-call(bf16[2048,640]{1,0:T(8,128)(2,1)} %bitcast.2, ...), custom_call_target="tpu_custom_call" | custom-call | tf_op jit(solution)/shard_map/step_kernel/pallas_call | solution.py:598
  200.3 152.6 %gather_kernel.1 = (bf16[2,640,2560]{2,1,0:T(8,128)(2,1)S(1)}, bf16[2,640,2560]{2,1,0:T(8,128)(2,1)S(1)}, bf16[2,2560,640]{2,1,0:T(8,128)(2,1)S(1)}, f32[2,80,25...) custom-call(f32[8,128]{1,0:T(8,128)} %get-tuple-element.30.ofac, ...), custom_call_target="tpu_custom_call" | custom-call | tf_op jit(solution)/shard_map/gather_kernel/pallas_call | solution.py:885
  352.9 9.9 %put_kernel.1 = (bf16[2,640,2560]{2,1,0:T(8,128)(2,1)}, bf16[2,640,2560]{2,1,0:T(8,128)(2,1)}, bf16[2,2560,640]{2,1,0:T(8,128)(2,1)}, f32[2,80,2560]{2,1,0:T(8,1...) custom-call(bf16[2,640,2560]{2,1,0:T(8,128)(2,1)S(1)} %get-tuple-ele, ...), custom_call_target="tpu_custom_call" | custom-call | tf_op jit(solution)/shard_map/put_kernel/pallas_call | solution.py:928
